TPU v7x, 32 devices: a whole 2x2x4 slice. The times are simulated.
32 devices in a mesh: dom: 8 (over z, y), rep: 4 (over x, core).
Axes of the slice: x: 2, y: 2, z: 4, core: 2. Of those that a mesh axis runs over, the one named last changes fastest.
Arguments:
- ns_shape: bfloat16 [64, 256], replicated, may hold values from -0.75 to 0.75
- nm_shape: bfloat16 [64, 256], replicated, may hold values from -0.75 to 0.75
- sec_disp: bfloat16 [64, 262144], P(None, ('dom', 'rep')), may hold values from -6 to 6
- mst_disp: bfloat16 [64, 262144], P(None, ('dom', 'rep')), may hold values from -6 to 6
- gap_offset: float32 [262144], P(('dom', 'rep')), may hold values from -6 to 6
- quad_weight: float32 [256], replicated, may hold values from 0.25 to 4
- jacobian: float32 [262144], P(('dom', 'rep')), may hold values from 0.0005 to 0.005
- segment_slot: int32 [262144], P(('dom', 'rep')), may hold values from 0 to 1279, as said below
- face_id: int32 [262144], P(('dom', 'rep')), may hold values from 0 to 1073741823
- search_rank: int32 [262144], P(('dom', 'rep')), may hold values from 0 to 3
- live_rows: int32 [32], P(('dom', 'rep')), may hold values from 1024 to 8192, as said below
Outputs:
- contact_force: bfloat16 [64, 262144], P(None, ('dom', 'rep'))
- seg_pen: float32 [8192], P('dom')
- seg_face: int32 [8192], P('dom')
- seg_gap: float32 [8192], P('dom')
- mean_gap: float32 [], replicated
Inputs may be any that keep to these rules, and one draw needn't show every extreme that they name: `segment_slot`: A row's segment is (1024 times the dom index of its device plus its slot) modulo 8192; slots of 1024 or more reach the next dom index's first 256 segments. `live_rows`: entry b counts the live rows of the device with flat index b (dom-major); they are that device's first rows, the rest are padding; some device is full in every draw.
All inputs are finite; a program needn't handle non-finite values.
Results may differ from a plain program's by a relative error of at most 0.0055.
Values sent between devices are 32-bit elements; how exact they have to be, the bound alone decides.
A program may use at most 64 MiB of HBM per device.

v0:
```python
import functools

import jax
import jax.numpy as jnp
from jax import lax
from jax.experimental import pallas as pl
from jax.experimental.pallas import tpu as pltpu
from jax.sharding import PartitionSpec as P

SEG_DEV = 1024
SPILL = 256
LANES = 128
SUB = 8
WIDTH = 64
PER_ROW = LANES // WIDTH
GROUPS = (SEG_DEV + SPILL) // WIDTH
OWN_GROUPS = SEG_DEV // WIDTH
SPILL_GROUPS = SPILL // WIDTH
OWN_ROWS = SEG_DEV // LANES
SPILL_ROWS = SPILL // LANES
ALL_ROWS = 16
CODE = 32

PENALTY = 400.0
LOWEST_FILL = -1e30
FACE_LIMIT = 1073741824
FACE_MASK = FACE_LIMIT - 1
KEY_LOW = -2147483648
MESH = pl.DeviceIdType.MESH
TILE = 256
DEPTH = 12
BATCH = 4
UNROLL = 16
CHAINS = 4
FORCE_UNROLL = 8
EXTRA = 16
VMEM_LIMIT = 32 << 20


def split3(x):
    a = x.astype(jnp.bfloat16)
    rest = x - a.astype(jnp.float32)
    b = rest.astype(jnp.bfloat16)
    c = (rest - b.astype(jnp.float32)).astype(jnp.bfloat16)
    return a, b, c


def row(ref, at):
    return ref[pl.ds(at, SUB, stride=0), :]


def pull_groups(first, count, depth0, depth, code_ref, sources, packs):
    all_lines = code_ref.shape[0]
    sub = lax.broadcasted_iota(jnp.int32, (SUB, LANES), 0)
    blocks = -(-count * depth // SUB)
    wants = []
    for b in range(blocks):
        line = sub + SUB * b
        want = jnp.full((SUB, LANES), -2, jnp.int32)
        for q in range(count):
            inside = (line >= q * depth) & (line < (q + 1) * depth)
            want = jnp.where(inside, (line + (depth0 - q * depth)) * CODE + (first + q), want)
        wants.append(want)
    fills = (-1, LOWEST_FILL, -1, 0.0)

    def pull(i, carry):
        parts = [list(part) for part in carry]
        code = row(code_ref, i)
        values = [row(ref, i) for ref in sources]
        for b in range(blocks):
            hit = code == wants[b]
            for part, value in zip(parts, values):
                part[b] = jnp.where(hit, value, part[b])
        return tuple(tuple(part) for part in parts)

    start = tuple(
        (jnp.full((SUB, LANES), fill, ref.dtype),) * blocks for fill, ref in zip(fills, sources)
    )
    pulled = lax.fori_loop(0, all_lines, pull, start, unroll=8)
    for ref, parts in zip(packs, pulled):
        for b in range(blocks):
            ref[SUB * b : SUB * (b + 1), :] = parts[b]


def match_group(g, at, depth, packs):
    sub = lax.broadcasted_iota(jnp.int32, (SUB, LANES), 0)
    tiles = WIDTH // SUB
    marks = [sub + (g * WIDTH + SUB * q) for q in range(tiles)]
    pens = [jnp.full((SUB, LANES), LOWEST_FILL, jnp.float32)] * tiles
    keys = [jnp.full((SUB, LANES), KEY_LOW, jnp.int32)] * tiles
    gaps = [jnp.zeros((SUB, LANES), jnp.float32)] * tiles
    for j in range(depth):
        slot, pen, key, gap = (row(ref, at + j) for ref in packs)
        for q in range(tiles):
            hit = slot == marks[q]
            pens[q] = jnp.maximum(pens[q], jnp.where(hit, pen, LOWEST_FILL))
            keys[q] = jnp.maximum(keys[q], jnp.where(hit, key, KEY_LOW))
            gaps[q] = gaps[q] + jnp.where(hit, gap, 0.0)
    return pens, keys, gaps


def across(parts):
    pens, keys, gaps = (jnp.concatenate(sum(lists, []), axis=0).T for lists in zip(*parts))
    return (
        jnp.max(pens, axis=0, keepdims=True),
        jnp.max(keys, axis=0, keepdims=True),
        jnp.sum(gaps, axis=0, keepdims=True),
    )


def project(wt, x_ref, off_ref, tile):
    cols = pl.ds(tile * TILE, TILE)
    per_tile = TILE // LANES
    offset = jnp.concatenate([row(off_ref, tile * per_tile + i) for i in range(per_tile)], axis=1)
    sub = lax.broadcasted_iota(jnp.int32, (SUB, TILE), 0)
    a, b, c = (part.astype(jnp.float32) for part in split3(offset))
    extra = jnp.where(sub == 0, a, jnp.where(sub == 1, b, jnp.where(sub == 2, c, 0.0)))
    extra = jnp.concatenate([extra, jnp.zeros((EXTRA - SUB, TILE), jnp.float32)], axis=0)
    x = jnp.concatenate([x_ref[:, cols], extra.astype(jnp.bfloat16)], axis=0)
    return jnp.dot(wt, x, preferred_element_type=jnp.float32)


def store_row(ref, tile, value):
    per_tile = TILE // LANES
    for i in range(per_tile):
        ref[pl.ds(tile * per_tile + i, 1), :] = value[:, i * LANES : (i + 1) * LANES]


def reduce_field(field, p_size, tile, pen_ref, gap_ref):
    low = [field[SUB * j : SUB * (j + 1)] for j in range(CHAINS)]
    for j in range(CHAINS, p_size // SUB):
        low[j % CHAINS] = jnp.minimum(low[j % CHAINS], field[SUB * j : SUB * (j + 1)])
    store_row(pen_ref, tile, -jnp.min(functools.reduce(jnp.minimum, low), axis=0, keepdims=True))
    store_row(gap_ref, tile, jnp.sum(field[p_size : p_size + SUB], axis=0, keepdims=True))


def prep_kernel(
    live_h, ns_h, nm_h, qw_h, sec_h, mst_h, off_h, jac_h, slot_h, face_h, rank_h,
    x_ref, wt_ref, nq_ref, off_ref, jl_ref, slot_ref, code_ref, key_ref, over_pen, over_key, over_gap, area_ref,
    live_s, ns_ref, nm_ref, qw_ref, jac_ref, face_ref, rank_ref, pen_ref, gap_ref, packs, s_small, s_big,
):
    lines = slot_ref.shape[0]
    k_size, p_size = ns_ref.shape
    rows = x_ref.shape[1]

    small = [
        pltpu.make_async_copy(source, held, s_small.at[i])
        for i, (source, held) in enumerate((
            (slot_h, slot_ref), (live_h, live_s), (ns_h, ns_ref), (nm_h, nm_ref), (qw_h, qw_ref),
            (face_h, face_ref), (rank_h, rank_ref), (jac_h, jac_ref), (off_h, off_ref),
        ))
    ]
    for copy in small:
        copy.start()
    for base, source in ((0, sec_h), (k_size, mst_h)):
        for at in range(0, k_size, 2 * SUB):
            pltpu.make_async_copy(
                source.at[at : at + 2 * SUB, :], x_ref.at[base + at : base + at + 2 * SUB, :], s_big
            ).start()
    for copy in small:
        copy.wait()

    row_id = (
        lax.broadcasted_iota(jnp.int32, (lines, LANES), 0) * LANES
        + lax.broadcasted_iota(jnp.int32, (lines, LANES), 1)
    )
    alive = row_id < live_s[...]
    group = jnp.where(alive, slot_ref[...] // WIDTH, -1)
    before = (
        lax.broadcasted_iota(jnp.int32, (lines, lines), 1)
        < lax.broadcasted_iota(jnp.int32, (lines, lines), 0)
    )
    before = jnp.where(before, 1.0, 0.0).astype(jnp.bfloat16)
    place = jnp.zeros((lines, LANES), jnp.float32)
    for g in range(0, GROUPS, 2):
        mine = [group == g, group == g + 1]
        seen = jnp.concatenate([jnp.where(m, 1.0, 0.0).astype(jnp.bfloat16) for m in mine], axis=1)
        found = jnp.dot(before, seen, preferred_element_type=jnp.float32)
        place = jnp.where(mine[0], found[:, :LANES], jnp.where(mine[1], found[:, LANES:], place))
    code = jnp.where(alive, place.astype(jnp.int32) * CODE + group, -1)
    code_ref[...] = code
    worst = jnp.max(code)

    w = jnp.concatenate([ns_ref[...], -nm_ref[...]], axis=0).astype(jnp.float32)
    qrow = qw_ref[...]
    wt = w.T
    qmat = jnp.broadcast_to(qrow, (LANES, p_size)).T
    v = jnp.sum(wt * qmat, axis=0, keepdims=True)
    qsum = jnp.sum(qmat, axis=0, keepdims=True)
    depth = wt_ref.shape[1]
    pick = lax.broadcasted_iota(jnp.int32, (EXTRA, depth), 0)
    column = lax.broadcasted_iota(jnp.int32, (p_size, depth - 2 * k_size), 1)
    wt_ref[0:p_size, 0 : 2 * k_size] = wt.astype(jnp.bfloat16)
    wt_ref[0:p_size, 2 * k_size :] = jnp.where(column < 3, 1.0, 0.0).astype(jnp.bfloat16)
    lane_row = lax.broadcasted_iota(jnp.int32, (1, LANES), 1)
    tail = jnp.where(lane_row < 3, qsum, 0.0)[:, : depth - 2 * k_size]
    a, b, c = (part.astype(jnp.float32) for part in split3(jnp.concatenate([v, tail], axis=1)))
    stacked = jnp.where(pick == 0, a, jnp.where(pick == 1, b, jnp.where(pick == 2, c, 0.0)))
    wt_ref[p_size:, :] = stacked.astype(jnp.bfloat16)
    scaled = ns_ref[...].astype(jnp.float32) * qrow
    top = scaled.astype(jnp.bfloat16)
    low = (scaled - top.astype(jnp.float32)).astype(jnp.bfloat16)
    nq_ref[...] = jnp.concatenate([top, low], axis=0)

    key_ref[...] = ((rank_ref[...] - 2) << 30) + (FACE_MASK - face_ref[...])
    jl = jnp.where(alive, jac_ref[...], 0.0)
    jl_ref[...] = jl
    area_ref[...] = jnp.sum(jl, axis=0, keepdims=True) * jnp.sum(qrow, axis=1, keepdims=True)
    over_pen[...] = jnp.full(over_pen.shape, LOWEST_FILL, jnp.float32)
    over_key[...] = jnp.full(over_key.shape, KEY_LOW, jnp.int32)
    over_gap[...] = jnp.zeros(over_gap.shape, jnp.float32)

    pltpu.make_async_copy(x_ref, x_ref, s_big).wait()

    @pl.when(worst >= DEPTH * CODE)
    def _():
        weights = wt_ref[...]

        def fill(tile, carry):
            reduce_field(project(weights, x_ref, off_ref, tile), p_size, tile, pen_ref, gap_ref)
            return carry

        lax.fori_loop(0, rows // TILE, fill, 0)
        gap_ref[...] = gap_ref[...] * jl_ref[...]
        face_ref[...] = code_ref[...]

        def one(worst):
            code = face_ref[...]
            g = worst & (CODE - 1)
            low = jnp.maximum((worst // CODE) & -SUB, DEPTH)
            pull_groups(g, 1, low, SUB, face_ref, (slot_ref, pen_ref, key_ref, gap_ref), packs)
            found = match_group(g, 0, SUB, packs)
            odd = jnp.full((SUB, LANES), g & 1, jnp.int32)
            fills = (LOWEST_FILL, KEY_LOW, 0.0)
            parts = [
                tuple([jnp.where(odd == side, x, fill) for x in part] for part, fill in zip(found, fills))
                for side in range(PER_ROW)
            ]
            pen, key, gap = across(parts)
            at = pl.ds(g // PER_ROW, 1)
            over_pen[at, :] = jnp.maximum(over_pen[at, :], pen)
            over_key[at, :] = jnp.maximum(over_key[at, :], key)
            over_gap[at, :] = over_gap[at, :] + gap
            done = ((code & (CODE - 1)) == g) & (code >= low * CODE)
            code = jnp.where(done, -1, code)
            face_ref[...] = code
            return jnp.max(code)

        lax.while_loop(lambda worst: worst >= DEPTH * CODE, one, worst)


def main_kernel(
    n_dom, n_rep,
    x_ref, wt_ref, nq_ref, off_ref, jl_ref, slot_ref, code_ref, key_ref, over_pen, over_key, over_gap, area_ref,
    force_ref, out_pen, out_face, out_gap, out_mean,
    load_ref, pen_ref, gap_ref, packs, raw_pen, raw_key, raw_gap,
    sp_sf, sp_si, ow_sf, ow_si, t1_s, t2_s, sp_f, sp_i, ow_f, ow_i, t1_d, t2_d,
    s_spf, r_spf, s_spi, r_spi, s_owf, r_owf, s_owi, r_owi, s_t1, r_t1, s_t2, r_t2, inside,
):
    dom = lax.axis_index("dom")
    rep = lax.axis_index("rep")
    k_size = force_ref.shape[0]
    rows = force_ref.shape[1]
    p_size = load_ref.shape[0]
    per_tile = TILE // LANES
    tiles = rows // TILE
    count = n_dom * n_rep
    me = dom * n_rep + rep

    def dev(d, r):
        return {"dom": lax.rem(d + n_dom, n_dom), "rep": lax.rem(r + n_rep, n_rep)}

    def flat_dev(flat):
        return dev(lax.div(flat, n_rep), lax.rem(flat, n_rep))

    barrier = pltpu.get_barrier_semaphore()

    def signal(sem, first, last):
        def one(flat, carry):
            pl.semaphore_signal(sem, inc=1, device_id=flat_dev(flat), device_id_type=MESH)
            return carry

        lax.fori_loop(first, last, one, 0)

    signal(barrier, me + 1, count)
    signal(barrier, dom * n_rep, me)
    signal(barrier, jnp.maximum(dom - 1, 0) * n_rep, dom * n_rep)

    wt = wt_ref[...]

    def wide_row(ref, tile):
        return jnp.concatenate([row(ref, tile * per_tile + i) for i in range(per_tile)], axis=1)

    def batch(step, carry):
        for i in range(UNROLL):
            tile = step * UNROLL + i
            cols = pl.ds(tile * TILE, TILE)
            field = project(wt, x_ref, off_ref, tile)
            for at in range(0, p_size, 2 * SUB):
                load_ref[at : at + 2 * SUB, cols] = jnp.minimum(field[at : at + 2 * SUB].astype(jnp.bfloat16), 0)
            reduce_field(field, p_size, tile, pen_ref, gap_ref)
        return carry

    lax.fori_loop(0, tiles // UNROLL, batch, 0)
    row_gap = gap_ref[...] * jl_ref[...]
    gap_ref[...] = row_gap
    total_gap = jnp.sum(jnp.sum(row_gap, axis=0, keepdims=True), axis=1, keepdims=True)
    total_area = jnp.sum(area_ref[...], axis=1, keepdims=True)
    lane = lax.broadcasted_iota(jnp.int32, (1, LANES), 1)
    t1_s[...] = jnp.where(lane == 0, total_gap, jnp.where(lane == 1, total_area, 0.0))

    after = n_rep * jnp.where(dom < n_dom - 1, 1, 0)
    pl.semaphore_wait(barrier, me + (n_rep - 1 - rep) + after)
    signal(inside, 0, me)

    mate = rep + 1 - 2 * lax.rem(rep, 2)
    first_copy = pltpu.make_async_remote_copy(
        src_ref=t1_s, dst_ref=t1_d, send_sem=s_t1, recv_sem=r_t1,
        device_id=dev(dom, mate), device_id_type=MESH,
    )
    first_copy.start()

    def scan(first, base):
        pull_groups(first, BATCH, 0, DEPTH, code_ref, (slot_ref, pen_ref, key_ref, gap_ref), packs)
        for i in range(BATCH // PER_ROW):
            parts = [
                match_group(first + i * PER_ROW + j, (i * PER_ROW + j) * DEPTH, DEPTH, packs) for j in range(PER_ROW)
            ]
            pen, key, gap = across(parts)
            over = pl.ds(first // PER_ROW + i, 1)
            at = pl.ds(base + i, 1)
            raw_pen[at, :] = jnp.maximum(pen, over_pen[over, :])
            raw_key[at, :] = jnp.maximum(key, over_key[over, :])
            raw_gap[at, :] = gap + over_gap[over, :]

    def decode(top, best):
        none = top < LOWEST_FILL * 0.5
        rank = jnp.where(none, -1, (best >> 30) + 2)
        face = jnp.where(none, FACE_LIMIT, FACE_MASK - (best & FACE_MASK))
        return rank, face

    scan(OWN_GROUPS, 0)
    part = slice(0, SPILL_ROWS)
    rank, face = decode(raw_pen[part, :], raw_key[part, :])
    sp_sf[0:SPILL_ROWS, :] = raw_pen[part, :]
    sp_sf[SPILL_ROWS:, :] = raw_gap[part, :]
    sp_si[0:SPILL_ROWS, :] = rank
    sp_si[SPILL_ROWS:, :] = face

    def spill_copy(j):
        where = dev(dom + 1, rep + j)
        return (
            pltpu.make_async_remote_copy(
                src_ref=sp_sf, dst_ref=sp_f.at[rep], send_sem=s_spf, recv_sem=r_spf,
                device_id=where, device_id_type=MESH,
            ),
            pltpu.make_async_remote_copy(
                src_ref=sp_si, dst_ref=sp_i.at[rep], send_sem=s_spi, recv_sem=r_spi,
                device_id=where, device_id_type=MESH,
            ),
        )

    for j in range(n_rep):
        for copy in spill_copy(j):
            copy.start()

    first_copy.wait_recv()
    pairs = count // 2
    pair = lax.div(me, 2)
    both = t1_s[...] + t1_d[...]
    t2_s[...] = both
    t2_d[pl.ds(pair, 1), :] = both

    def send_pairs(first, last):
        def one(other, carry):
            pltpu.make_async_remote_copy(
                src_ref=t2_s, dst_ref=t2_d.at[pl.ds(pair, 1), :], send_sem=s_t2, recv_sem=r_t2,
                device_id=flat_dev(other * 2 + lax.rem(rep, 2)), device_id_type=MESH,
            ).start()
            return carry

        lax.fori_loop(first, last, one, 0)

    send_pairs(0, pair)

    def own_scan(i, carry):
        scan(i * BATCH, i * (BATCH // PER_ROW))
        return carry

    lax.fori_loop(0, OWN_GROUPS // BATCH, own_scan, 0)
    rank, face = decode(raw_pen[...], raw_key[...])
    ow_sf[0] = raw_pen[...]
    ow_sf[1] = raw_gap[...]
    ow_si[0] = rank
    ow_si[1] = face

    def own_copy(j):
        where = dev(dom, rep + j)
        return (
            pltpu.make_async_remote_copy(
                src_ref=ow_sf, dst_ref=ow_f.at[rep], send_sem=s_owf, recv_sem=r_owf,
                device_id=where, device_id_type=MESH,
            ),
            pltpu.make_async_remote_copy(
                src_ref=ow_si, dst_ref=ow_i.at[rep], send_sem=s_owi, recv_sem=r_owi,
                device_id=where, device_id_type=MESH,
            ),
        )

    for j in range(1, n_rep):
        for copy in own_copy(j):
            copy.start()
    ow_f[rep] = ow_sf[...]
    ow_i[rep] = ow_si[...]

    nq = nq_ref[...]

    def push(step, carry):
        for i in range(FORCE_UNROLL):
            tile = step * FORCE_UNROLL + i
            cols = pl.ds(tile * TILE, TILE)
            force = jnp.dot(nq, load_ref[:, cols], preferred_element_type=jnp.float32)
            scale = wide_row(jl_ref, tile)[0:1] * -PENALTY
            force_ref[:, cols] = ((force[:k_size] + force[k_size:]) * scale).astype(jnp.bfloat16)
        return carry

    lax.fori_loop(0, tiles // FORCE_UNROLL, push, 0)

    @pl.when(me < count - 1)
    def _():
        pl.semaphore_wait(inside, count - 1 - me)

    send_pairs(pair + 1, pairs)

    def encode(rank, face):
        return jnp.where(rank < 0, KEY_LOW, ((rank - 2) << 30) + (FACE_MASK - face))

    def settle(ref, sem):
        pltpu.make_async_copy(ref, ref, sem).wait()

    settle(ow_f.at[pl.ds(0, n_rep - 1)], r_owf)
    settle(ow_i.at[pl.ds(0, n_rep - 1)], r_owi)
    pen_o, gap_o = ow_f[0, 0], ow_f[0, 1]
    key_o = encode(ow_i[0, 0], ow_i[0, 1])
    for r in range(1, n_rep):
        pen_o = jnp.maximum(pen_o, ow_f[r, 0])
        gap_o = gap_o + ow_f[r, 1]
        key_o = jnp.maximum(key_o, encode(ow_i[r, 0], ow_i[r, 1]))

    settle(sp_f, s_spf)
    settle(sp_i, s_spi)
    settle(ow_f.at[pl.ds(0, n_rep - 1)], s_owf)
    settle(ow_i.at[pl.ds(0, n_rep - 1)], s_owi)
    first_copy.wait_send()
    settle(t2_d.at[pl.ds(0, pairs - 1), :], s_t2)

    settle(t2_d.at[pl.ds(0, pairs - 1), :], r_t2)
    whole = jnp.sum(t2_d[...], axis=0, keepdims=True)
    out_mean[...] = whole[:, 0:1] / whole[:, 1:2]

    settle(sp_f, r_spf)
    settle(sp_i, r_spi)
    g = SPILL_ROWS
    pen_s, gap_s = sp_f[0, 0:g], sp_f[0, g:]
    key_s = encode(sp_i[0, 0:g], sp_i[0, g:])
    for r in range(1, n_rep):
        pen_s = jnp.maximum(pen_s, sp_f[r, 0:g])
        gap_s = gap_s + sp_f[r, g:]
        key_s = jnp.maximum(key_s, encode(sp_i[r, 0:g], sp_i[r, g:]))

    def finish(at, pen, key, gap):
        none = pen < LOWEST_FILL * 0.5
        out_pen[at, :] = jnp.where(none, 0.0, pen)
        out_face[at, :] = jnp.where(none, -1, FACE_MASK - (key & FACE_MASK))
        out_gap[at, :] = jnp.where(none, 0.0, gap)

    finish(
        slice(0, g), jnp.maximum(pen_o[:g], pen_s), jnp.maximum(key_o[:g], key_s), gap_o[:g] + gap_s
    )
    finish(slice(g, OWN_ROWS), pen_o[g:], key_o[g:], gap_o[g:])


def finish_kernel(force_ref, pen_ref, face_ref, gap_ref, mean_ref, force_h, pen_h, face_h, gap_h, mean_h, sems, s_force):
    copies = [
        pltpu.make_async_copy(held, out, sems.at[i])
        for i, (held, out) in enumerate((
            (pen_ref, pen_h), (face_ref, face_h), (gap_ref, gap_h), (mean_ref, mean_h)
        ))
    ]
    for at in range(0, force_ref.shape[0], SUB):
        part = (slice(at, at + SUB), slice(None))
        pltpu.make_async_copy(force_ref.at[part], force_h.at[part], s_force).start()
    for copy in copies:
        copy.start()
    for copy in copies:
        copy.wait()
    pltpu.make_async_copy(force_ref, force_h, s_force).wait()


def solution(mesh):
    n_dom, n_rep = mesh.shape["dom"], mesh.shape["rep"]
    vmem = pl.BlockSpec(memory_space=pltpu.VMEM)
    anywhere = pl.BlockSpec(memory_space=pl.ANY)
    dma = pltpu.SemaphoreType.DMA

    def kept(x):
        return pltpu.with_memory_space_constraint(x, pltpu.VMEM)

    def streamed(x):
        return pltpu.with_memory_space_constraint(x, pltpu.HBM)

    def shards(ns, nm, sec, mst, off, qw, jac, slot, face, rank, live):
        k_size, p_size = ns.shape
        rows = sec.shape[1]
        lines = rows // LANES
        depth = 2 * k_size + EXTRA
        f32, i32, bf16 = jnp.float32, jnp.int32, jnp.bfloat16

        off, jac, slot, face, rank = (x.reshape(lines, LANES) for x in (off, jac, slot, face, rank))

        def packs(deep):
            return [pltpu.VMEM((deep + SUB, LANES), t) for t in (i32, f32, i32, f32)]

        held = pl.pallas_call(
            prep_kernel,
            out_shape=(
                pltpu.VMEM((2 * k_size, rows), bf16),
                pltpu.VMEM((p_size + EXTRA, depth), bf16),
                pltpu.VMEM((2 * k_size, p_size), bf16),
                pltpu.VMEM((lines, LANES), f32),
                pltpu.VMEM((lines, LANES), f32),
                pltpu.VMEM((lines, LANES), i32),
                pltpu.VMEM((lines, LANES), i32),
                pltpu.VMEM((lines, LANES), i32),
                pltpu.VMEM((ALL_ROWS, LANES), f32),
                pltpu.VMEM((ALL_ROWS, LANES), i32),
                pltpu.VMEM((ALL_ROWS, LANES), f32),
                pltpu.VMEM((1, LANES), f32),
            ),
            in_specs=[anywhere] * 11,
            out_specs=(vmem,) * 12,
            scratch_shapes=[
                pltpu.VMEM((1, 1), i32),
                pltpu.VMEM((k_size, p_size), bf16),
                pltpu.VMEM((k_size, p_size), bf16),
                pltpu.VMEM((1, p_size), f32),
                pltpu.VMEM((lines, LANES), f32),
                pltpu.VMEM((lines, LANES), i32),
                pltpu.VMEM((lines, LANES), i32),
                pltpu.VMEM((lines, LANES), f32),
                pltpu.VMEM((lines, LANES), f32),
                packs(SUB),
                dma((9,)),
                dma,
            ],
            compiler_params=pltpu.CompilerParams(vmem_limit_bytes=VMEM_LIMIT),
        )(
            live.reshape(1, 1),
            *(streamed(x) for x in (ns, nm, qw.reshape(1, p_size), sec, mst, off, jac, slot, face, rank)),
        )

        spill = (2 * SPILL_ROWS, LANES)
        own = (2, OWN_ROWS, LANES)
        pairs = n_dom * n_rep // 2
        results = pl.pallas_call(
            functools.partial(main_kernel, n_dom, n_rep),
            out_shape=(
                pltpu.VMEM((k_size, rows), bf16),
                pltpu.VMEM((OWN_ROWS, LANES), f32),
                pltpu.VMEM((OWN_ROWS, LANES), i32),
                pltpu.VMEM((OWN_ROWS, LANES), f32),
                pltpu.VMEM((1, 1), f32),
            ),
            in_specs=[vmem] * 12,
            out_specs=(vmem,) * 5,
            scratch_shapes=[
                pltpu.VMEM((p_size, rows), bf16),
                pltpu.VMEM((lines, LANES), f32),
                pltpu.VMEM((lines, LANES), f32),
                packs(BATCH * DEPTH),
                pltpu.VMEM((OWN_ROWS, LANES), f32),
                pltpu.VMEM((OWN_ROWS, LANES), i32),
                pltpu.VMEM((OWN_ROWS, LANES), f32),
                pltpu.VMEM(spill, f32),
                pltpu.VMEM(spill, i32),
                pltpu.VMEM(own, f32),
                pltpu.VMEM(own, i32),
                pltpu.VMEM((1, LANES), f32),
                pltpu.VMEM((1, LANES), f32),
                pltpu.VMEM((n_rep,) + spill, f32),
                pltpu.VMEM((n_rep,) + spill, i32),
                pltpu.VMEM((n_rep,) + own, f32),
                pltpu.VMEM((n_rep,) + own, i32),
                pltpu.VMEM((1, LANES), f32),
                pltpu.VMEM((pairs, LANES), f32),
            ] + [dma] * 12 + [pltpu.SemaphoreType.REGULAR],
            compiler_params=pltpu.CompilerParams(
                collective_id=0, has_side_effects=True, vmem_limit_bytes=VMEM_LIMIT
            ),
        )(*(kept(x) for x in held))

        force, seg_pen, seg_face, seg_gap, mean = pl.pallas_call(
            finish_kernel,
            out_shape=tuple(jax.ShapeDtypeStruct(x.shape, x.dtype) for x in results),
            in_specs=[vmem] * 5,
            out_specs=(anywhere,) * 5,
            scratch_shapes=[dma((4,)), dma],
            compiler_params=pltpu.CompilerParams(vmem_limit_bytes=VMEM_LIMIT),
        )(*(kept(x) for x in results))
        seg_pen, seg_face, seg_gap = (x.reshape(SEG_DEV) for x in (seg_pen, seg_face, seg_gap))
        return force, seg_pen, seg_face, seg_gap, mean.reshape(())

    rows_spec, wide_spec = P(("dom", "rep")), P(None, ("dom", "rep"))
    return jax.shard_map(
        shards,
        mesh=mesh,
        in_specs=(P(), P(), wide_spec, wide_spec, rows_spec, P()) + (rows_spec,) * 5,
        out_specs=(wide_spec, P("dom"), P("dom"), P("dom"), P()),
        check_vma=False,
    )
```

profile of v0, /device:TPU:24, one launch (start us, length us, event | category | flops | bytes accessed | tf_op | source)
XLA Modules:
  0.0 18.5 jit_solution(2509467346842064588)
XLA Ops:
  1.3 2.1 %shard_map.146 = (bf16[128,8192]{1,0:T(8,128)(2,1)S(1)}, bf16[272,144]{1,0:T(8,128)(2,1)S(1)}, bf16[128,256]{1,0:T(8,128)(2,1)S(1)}, f32[64,128]{1,0:T(8,128)S(1...) custom-call(s32[1,1]{1,0:T(1,128)} %bitcast.11.live_h, ...), custom_call_target="tpu_custom_call" | custom-call | tf_op jit(solution)/shard_map/pallas_call | solution.py:524
  3.4 13.5 %shard_map.147 = (bf16[64,8192]{1,0:T(8,128)(2,1)S(1)}, f32[8,128]{1,0:T(8,128)S(1)}, s32[8,128]{1,0:T(8,128)S(1)}, f32[8,128]{1,0:T(8,128)S(1)}, f32[1,1]{1,0:T(1,128)}) custom-call(bf16[128,8192]{1,0:T(8,128)(2,1)S(1)} %get-tuple-element.27.x_ref, bf16[272,144]{1,0:T(8,128)(2,1)S(1)} %get-tuple-element.28.wt_ref, ...), custom_call_target="tpu_custom_call" | custom-call | tf_op jit(solution)/shard_map/pallas_call | solution.py:565
  16.9 1.6 %shard_map.148 = (bf16[64,8192]{1,0:T(8,128)(2,1)}, f32[8,128]{1,0:T(8,128)}, s32[8,128]{1,0:T(8,128)}, f32[8,128]{1,0:T(8,128)}, f32[1,1]{1,0:T(1,128)}) custom-call(bf16[64,8192]{1,0:T(8,128)(2,1)S(1)} %get-tuple-element.39.force_ref, f32[8,128]{1,0:T(8,128)S(1)} %get-tuple-element.40.pen_ref, s32[8,128]{1,0:T(8,128)S(1)} %get-tuple-element.41.face_ref, ...), custom_call_target="tpu_custom_call" | custom-call | tf_op jit(solution)/shard_map/pallas_call | solution.py:602
where the time goes:
time: 18.7 us; the launch traced here: 18.5 us
  Pallas kernels  17.2 us (92%)
  between operations  1.3 us (7%)
    pallas_call x1, Pallas kernels, shards(): pl.pallas_call(functools.partial(main_kernel, n_dom, n_rep), out_shape=(p...  13.5 us
    pallas_call x1, Pallas kernels, shards(): pl.pallas_call(prep_kernel, out_shape=(pltpu.VMEM((2 * k_size, rows), bf1...  2.11 us
    pallas_call x1, Pallas kernels, shards(): pl.pallas_call(finish_kernel, out_shape=tuple((jax.ShapeDtypeStruct(x.sha...  1.64 us

commit v1 on v0

--- a/solution.py
+++ b/solution.py
@@ -33,6 +33,7 @@
 UNROLL = 16
 CHAINS = 4
 FORCE_UNROLL = 8
+LOOP_UNROLL = 4
 EXTRA = 16
 VMEM_LIMIT = 32 << 20
 
@@ -82,25 +83,42 @@
             ref[SUB * b : SUB * (b + 1), :] = parts[b]
 
 
-def match_group(g, at, depth, packs):
+def match_group(g, at, depth, packs, unroll):
     sub = lax.broadcasted_iota(jnp.int32, (SUB, LANES), 0)
     tiles = WIDTH // SUB
     marks = [sub + (g * WIDTH + SUB * q) for q in range(tiles)]
-    pens = [jnp.full((SUB, LANES), LOWEST_FILL, jnp.float32)] * tiles
-    keys = [jnp.full((SUB, LANES), KEY_LOW, jnp.int32)] * tiles
-    gaps = [jnp.zeros((SUB, LANES), jnp.float32)] * tiles
-    for j in range(depth):
+    start = (
+        (jnp.full((SUB, LANES), LOWEST_FILL, jnp.float32),) * tiles,
+        (jnp.full((SUB, LANES), KEY_LOW, jnp.int32),) * tiles,
+        (jnp.zeros((SUB, LANES), jnp.float32),) * tiles,
+    )
+
+    def one(j, carry):
+        pens, keys, gaps = (list(part) for part in carry)
         slot, pen, key, gap = (row(ref, at + j) for ref in packs)
         for q in range(tiles):
             hit = slot == marks[q]
             pens[q] = jnp.maximum(pens[q], jnp.where(hit, pen, LOWEST_FILL))
             keys[q] = jnp.maximum(keys[q], jnp.where(hit, key, KEY_LOW))
             gaps[q] = gaps[q] + jnp.where(hit, gap, 0.0)
-    return pens, keys, gaps
-
-
-def across(parts):
-    pens, keys, gaps = (jnp.concatenate(sum(lists, []), axis=0).T for lists in zip(*parts))
+        return tuple(pens), tuple(keys), tuple(gaps)
+
+    if unroll == depth:
+        for j in range(depth):
+            start = one(j, start)
+        return start
+    return lax.fori_loop(0, depth, one, start, unroll=unroll)
+
+
+def keep_group(accs, side, parts):
+    for ref, part in zip(accs, parts):
+        for q in range(WIDTH // SUB):
+            at = side * WIDTH + q * SUB
+            ref[at : at + SUB, :] = part[q]
+
+
+def across(accs):
+    pens, keys, gaps = (ref[...].T for ref in accs)
     return (
         jnp.max(pens, axis=0, keepdims=True),
         jnp.max(keys, axis=0, keepdims=True),
@@ -137,7 +155,7 @@
 def prep_kernel(
     live_h, ns_h, nm_h, qw_h, sec_h, mst_h, off_h, jac_h, slot_h, face_h, rank_h,
     x_ref, wt_ref, nq_ref, off_ref, jl_ref, slot_ref, code_ref, key_ref, over_pen, over_key, over_gap, area_ref,
-    live_s, ns_ref, nm_ref, qw_ref, jac_ref, face_ref, rank_ref, pen_ref, gap_ref, packs, s_small, s_big,
+    live_s, ns_ref, nm_ref, qw_ref, jac_ref, face_ref, rank_ref, pen_ref, gap_ref, packs, accs, s_small, s_big,
 ):
     lines = slot_ref.shape[0]
     k_size, p_size = ns_ref.shape
@@ -229,14 +247,14 @@
             g = worst & (CODE - 1)
             low = jnp.maximum((worst // CODE) & -SUB, DEPTH)
             pull_groups(g, 1, low, SUB, face_ref, (slot_ref, pen_ref, key_ref, gap_ref), packs)
-            found = match_group(g, 0, SUB, packs)
+            found = match_group(g, 0, SUB, packs, 2)
             odd = jnp.full((SUB, LANES), g & 1, jnp.int32)
-            fills = (LOWEST_FILL, KEY_LOW, 0.0)
-            parts = [
-                tuple([jnp.where(odd == side, x, fill) for x in part] for part, fill in zip(found, fills))
-                for side in range(PER_ROW)
-            ]
-            pen, key, gap = across(parts)
+            for side in range(PER_ROW):
+                keep_group(accs, side, [
+                    [jnp.where(odd == side, x, fill) for x in part]
+                    for part, fill in zip(found, (LOWEST_FILL, KEY_LOW, 0.0))
+                ])
+            pen, key, gap = across(accs)
             at = pl.ds(g // PER_ROW, 1)
             over_pen[at, :] = jnp.maximum(over_pen[at, :], pen)
             over_key[at, :] = jnp.maximum(over_key[at, :], key)
@@ -253,7 +271,7 @@
     n_dom, n_rep,
     x_ref, wt_ref, nq_ref, off_ref, jl_ref, slot_ref, code_ref, key_ref, over_pen, over_key, over_gap, area_ref,
     force_ref, out_pen, out_face, out_gap, out_mean,
-    load_ref, pen_ref, gap_ref, packs, raw_pen, raw_key, raw_gap,
+    load_ref, pen_ref, gap_ref, packs, even_accs, odd_accs, raw_pen, raw_key, raw_gap,
     sp_sf, sp_si, ow_sf, ow_si, t1_s, t2_s, sp_f, sp_i, ow_f, ow_i, t1_d, t2_d,
     s_spf, r_spf, s_spi, r_spi, s_owf, r_owf, s_owi, r_owi, s_t1, r_t1, s_t2, r_t2, inside,
 ):
@@ -320,18 +338,22 @@
     )
     first_copy.start()
 
-    def scan(first, base):
+    def pull_batch(first):
         pull_groups(first, BATCH, 0, DEPTH, code_ref, (slot_ref, pen_ref, key_ref, gap_ref), packs)
-        for i in range(BATCH // PER_ROW):
-            parts = [
-                match_group(first + i * PER_ROW + j, (i * PER_ROW + j) * DEPTH, DEPTH, packs) for j in range(PER_ROW)
-            ]
-            pen, key, gap = across(parts)
-            over = pl.ds(first // PER_ROW + i, 1)
-            at = pl.ds(base + i, 1)
-            raw_pen[at, :] = jnp.maximum(pen, over_pen[over, :])
-            raw_key[at, :] = jnp.maximum(key, over_key[over, :])
-            raw_gap[at, :] = gap + over_gap[over, :]
+
+    def match_pair(first, i, accs, last_accs, over, at):
+        g = first + i * PER_ROW
+        keep_group(accs, 0, match_group(g, i * PER_ROW * DEPTH, DEPTH, packs, LOOP_UNROLL))
+        if last_accs is not None:
+            close_pair(last_accs, over, at)
+        keep_group(accs, 1, match_group(g + 1, (i * PER_ROW + 1) * DEPTH, DEPTH, packs, DEPTH))
+
+    def close_pair(accs, over, at):
+        pen, key, gap = across(accs)
+        over, at = pl.ds(over, 1), pl.ds(at, 1)
+        raw_pen[at, :] = jnp.maximum(pen, over_pen[over, :])
+        raw_key[at, :] = jnp.maximum(key, over_key[over, :])
+        raw_gap[at, :] = gap + over_gap[over, :]
 
     def decode(top, best):
         none = top < LOWEST_FILL * 0.5
@@ -339,7 +361,10 @@
         face = jnp.where(none, FACE_LIMIT, FACE_MASK - (best & FACE_MASK))
         return rank, face
 
-    scan(OWN_GROUPS, 0)
+    pull_batch(OWN_GROUPS)
+    match_pair(OWN_GROUPS, 0, even_accs, None, 0, 0)
+    match_pair(OWN_GROUPS, 1, odd_accs, even_accs, OWN_ROWS, 0)
+    close_pair(odd_accs, OWN_ROWS + 1, 1)
     part = slice(0, SPILL_ROWS)
     rank, face = decode(raw_pen[part, :], raw_key[part, :])
     sp_sf[0:SPILL_ROWS, :] = raw_pen[part, :]
@@ -383,11 +408,29 @@
 
     send_pairs(0, pair)
 
+    def send_up():
+        @pl.when(me < count - 1)
+        def _():
+            pl.semaphore_wait(inside, count - 1 - me)
+
+        send_pairs(pair + 1, pairs)
+
+    late = me >= count // 2
+
+    @pl.when(late)
+    def _():
+        send_up()
+
     def own_scan(i, carry):
-        scan(i * BATCH, i * (BATCH // PER_ROW))
+        first = i * BATCH
+        last = lax.rem(2 * i + OWN_ROWS - 1, OWN_ROWS)
+        pull_batch(first)
+        match_pair(first, 0, even_accs, odd_accs, last, last)
+        match_pair(first, 1, odd_accs, even_accs, 2 * i, 2 * i)
         return carry
 
     lax.fori_loop(0, OWN_GROUPS // BATCH, own_scan, 0)
+    close_pair(odd_accs, OWN_ROWS - 1, OWN_ROWS - 1)
     rank, face = decode(raw_pen[...], raw_key[...])
     ow_sf[0] = raw_pen[...]
     ow_sf[1] = raw_gap[...]
@@ -413,6 +456,10 @@
     ow_f[rep] = ow_sf[...]
     ow_i[rep] = ow_si[...]
 
+    @pl.when(jnp.logical_not(late))
+    def _():
+        send_up()
+
     nq = nq_ref[...]
 
     def push(step, carry):
@@ -425,12 +472,6 @@
         return carry
 
     lax.fori_loop(0, tiles // FORCE_UNROLL, push, 0)
-
-    @pl.when(me < count - 1)
-    def _():
-        pl.semaphore_wait(inside, count - 1 - me)
-
-    send_pairs(pair + 1, pairs)
 
     def encode(rank, face):
         return jnp.where(rank < 0, KEY_LOW, ((rank - 2) << 30) + (FACE_MASK - face))
@@ -520,6 +561,9 @@
 
         def packs(deep):
             return [pltpu.VMEM((deep + SUB, LANES), t) for t in (i32, f32, i32, f32)]
+
+        def lanes():
+            return [pltpu.VMEM((LANES, LANES), t) for t in (f32, i32, f32)]
 
         held = pl.pallas_call(
             prep_kernel,
@@ -550,6 +594,7 @@
                 pltpu.VMEM((lines, LANES), f32),
                 pltpu.VMEM((lines, LANES), f32),
                 packs(SUB),
+                lanes(),
                 dma((9,)),
                 dma,
             ],
@@ -578,6 +623,8 @@
                 pltpu.VMEM((lines, LANES), f32),
                 pltpu.VMEM((lines, LANES), f32),
                 packs(BATCH * DEPTH),
+                lanes(),
+                lanes(),
                 pltpu.VMEM((OWN_ROWS, LANES), f32),
                 pltpu.VMEM((OWN_ROWS, LANES), i32),
                 pltpu.VMEM((OWN_ROWS, LANES), f32),

time: 18.7 us -> 18.1 us (0.968)
  the two profiles are of different devices: /device:TPU:24 before, /device:TPU:0 now
where the time goes in v1:
time: 18.1 us; the launch traced here: 17.9 us
  Pallas kernels  16.6 us (92%)
  between operations  1.3 us (7%)
    pallas_call x1, Pallas kernels, shards(): pl.pallas_call(functools.partial(main_kernel, n_dom, n_rep), out_shape=(p...  12.9 us
    pallas_call x1, Pallas kernels, shards(): pl.pallas_call(prep_kernel, out_shape=(pltpu.VMEM((2 * k_size, rows), bf1...  2.11 us
    pallas_call x1, Pallas kernels, shards(): pl.pallas_call(finish_kernel, out_shape=tuple((jax.ShapeDtypeStruct(x.sha...  1.64 us

profile of v1, /device:TPU:0, one launch (start us, length us, event | category | flops | bytes accessed | tf_op | source)
XLA Modules:
  0.0 17.9 jit_solution(5769645635415592128)
XLA Ops:
  1.3 2.1 %shard_map.146 = (bf16[128,8192]{1,0:T(8,128)(2,1)S(1)}, bf16[272,144]{1,0:T(8,128)(2,1)S(1)}, bf16[128,256]{1,0:T(8,128)(2,1)S(1)}, f32[64,128]{1,0:T(8,128)S(1...) custom-call(s32[1,1]{1,0:T(1,128)} %bitcast.11.live_h, ...), custom_call_target="tpu_custom_call" | custom-call | tf_op jit(solution)/shard_map/pallas_call | solution.py:568
  3.4 12.9 %shard_map.147 = (bf16[64,8192]{1,0:T(8,128)(2,1)S(1)}, f32[8,128]{1,0:T(8,128)S(1)}, s32[8,128]{1,0:T(8,128)S(1)}, f32[8,128]{1,0:T(8,128)S(1)}, f32[1,1]{1,0:T(1,128)}) custom-call(bf16[128,8192]{1,0:T(8,128)(2,1)S(1)} %get-tuple-element.27.x_ref, bf16[272,144]{1,0:T(8,128)(2,1)S(1)} %get-tuple-element.28.wt_ref, ...), custom_call_target="tpu_custom_call" | custom-call | tf_op jit(solution)/shard_map/pallas_call | solution.py:610
  16.3 1.6 %shard_map.148 = (bf16[64,8192]{1,0:T(8,128)(2,1)}, f32[8,128]{1,0:T(8,128)}, s32[8,128]{1,0:T(8,128)}, f32[8,128]{1,0:T(8,128)}, f32[1,1]{1,0:T(1,128)}) custom-call(bf16[64,8192]{1,0:T(8,128)(2,1)S(1)} %get-tuple-element.39.force_ref, f32[8,128]{1,0:T(8,128)S(1)} %get-tuple-element.40.pen_ref, s32[8,128]{1,0:T(8,128)S(1)} %get-tuple-element.41.face_ref, ...), custom_call_target="tpu_custom_call" | custom-call | tf_op jit(solution)/shard_map/pallas_call | solution.py:649

commit v2 on v1

--- a/solution.py
+++ b/solution.py
@@ -30,6 +30,7 @@
 TILE = 256
 DEPTH = 12
 BATCH = 4
+OWN_BATCHES = OWN_GROUPS // BATCH
 UNROLL = 16
 CHAINS = 4
 FORCE_UNROLL = 8
@@ -174,7 +175,7 @@
         for at in range(0, k_size, 2 * SUB):
             pltpu.make_async_copy(
                 source.at[at : at + 2 * SUB, :], x_ref.at[base + at : base + at + 2 * SUB, :], s_big
-            ).start()
+            ).start(priority=1)
     for copy in small:
         copy.wait()
 
@@ -309,7 +310,18 @@
     def wide_row(ref, tile):
         return jnp.concatenate([row(ref, tile * per_tile + i) for i in range(per_tile)], axis=1)
 
+    last_dom = dom == n_dom - 1
+
+    def enter():
+        after = n_rep * jnp.where(last_dom, 0, 1)
+        pl.semaphore_wait(barrier, me + (n_rep - 1 - rep) + after)
+        signal(inside, 0, me)
+
     def batch(step, carry):
+        @pl.when(last_dom & (step == 1))
+        def _():
+            enter()
+
         for i in range(UNROLL):
             tile = step * UNROLL + i
             cols = pl.ds(tile * TILE, TILE)
@@ -327,9 +339,9 @@
     lane = lax.broadcasted_iota(jnp.int32, (1, LANES), 1)
     t1_s[...] = jnp.where(lane == 0, total_gap, jnp.where(lane == 1, total_area, 0.0))
 
-    after = n_rep * jnp.where(dom < n_dom - 1, 1, 0)
-    pl.semaphore_wait(barrier, me + (n_rep - 1 - rep) + after)
-    signal(inside, 0, me)
+    @pl.when(jnp.logical_not(last_dom))
+    def _():
+        enter()
 
     mate = rep + 1 - 2 * lax.rem(rep, 2)
     first_copy = pltpu.make_async_remote_copy(
@@ -415,13 +427,14 @@
 
         send_pairs(pair + 1, pairs)
 
-    late = me >= count // 2
-
-    @pl.when(late)
-    def _():
-        send_up()
+    quarter = lax.div(me * 4, count)
+    turn = OWN_BATCHES - quarter - jnp.where(quarter >= 2, 1, 0)
 
     def own_scan(i, carry):
+        @pl.when(i == turn)
+        def _():
+            send_up()
+
         first = i * BATCH
         last = lax.rem(2 * i + OWN_ROWS - 1, OWN_ROWS)
         pull_batch(first)
@@ -429,7 +442,7 @@
         match_pair(first, 1, odd_accs, even_accs, 2 * i, 2 * i)
         return carry
 
-    lax.fori_loop(0, OWN_GROUPS // BATCH, own_scan, 0)
+    lax.fori_loop(0, OWN_BATCHES, own_scan, 0)
     close_pair(odd_accs, OWN_ROWS - 1, OWN_ROWS - 1)
     rank, face = decode(raw_pen[...], raw_key[...])
     ow_sf[0] = raw_pen[...]
@@ -456,7 +469,7 @@
     ow_f[rep] = ow_sf[...]
     ow_i[rep] = ow_si[...]
 
-    @pl.when(jnp.logical_not(late))
+    @pl.when(turn >= OWN_BATCHES)
     def _():
         send_up()
 

time: 18.1 us -> 17.8 us (0.983)
  Pallas kernels: 16.6 us -> 16.3 us
    pallas_call x1, Pallas kernels: 2.11 us -> 1.71 us  [shards(): pl.pallas_call(prep_kernel, out_shape=(pltpu.VMEM((2 * k_size, rows), bf1...]
where the time goes in v2:
time: 17.8 us; the launch traced here: 17.6 us
  Pallas kernels  16.3 us (92%)
  between operations  1.3 us (7%)
    pallas_call x1, Pallas kernels, shards(): pl.pallas_call(functools.partial(main_kernel, n_dom, n_rep), out_shape=(p...  12.9 us
    pallas_call x1, Pallas kernels, shards(): pl.pallas_call(prep_kernel, out_shape=(pltpu.VMEM((2 * k_size, rows), bf1...  1.71 us
    pallas_call x1, Pallas kernels, shards(): pl.pallas_call(finish_kernel, out_shape=tuple((jax.ShapeDtypeStruct(x.sha...  1.64 us

profile of v2, /device:TPU:0, one launch (start us, length us, event | category | flops | bytes accessed | tf_op | source)
XLA Modules:
  0.0 17.6 jit_solution(162399859050596105)
XLA Ops:
  1.3 1.7 %shard_map.146 = (bf16[128,8192]{1,0:T(8,128)(2,1)S(1)}, bf16[272,144]{1,0:T(8,128)(2,1)S(1)}, bf16[128,256]{1,0:T(8,128)(2,1)S(1)}, f32[64,128]{1,0:T(8,128)S(1...) custom-call(s32[1,1]{1,0:T(1,128)} %bitcast.11.live_h, ...), custom_call_target="tpu_custom_call" | custom-call | tf_op jit(solution)/shard_map/pallas_call | solution.py:581
  3.0 12.9 %shard_map.147 = (bf16[64,8192]{1,0:T(8,128)(2,1)S(1)}, f32[8,128]{1,0:T(8,128)S(1)}, s32[8,128]{1,0:T(8,128)S(1)}, f32[8,128]{1,0:T(8,128)S(1)}, f32[1,1]{1,0:T(1,128)}) custom-call(bf16[128,8192]{1,0:T(8,128)(2,1)S(1)} %get-tuple-element.27.x_ref, bf16[272,144]{1,0:T(8,128)(2,1)S(1)} %get-tuple-element.28.wt_ref, ...), custom_call_target="tpu_custom_call" | custom-call | tf_op jit(solution)/shard_map/pallas_call | solution.py:623
  16.0 1.6 %shard_map.148 = (bf16[64,8192]{1,0:T(8,128)(2,1)}, f32[8,128]{1,0:T(8,128)}, s32[8,128]{1,0:T(8,128)}, f32[8,128]{1,0:T(8,128)}, f32[1,1]{1,0:T(1,128)}) custom-call(bf16[64,8192]{1,0:T(8,128)(2,1)S(1)} %get-tuple-element.39.force_ref, f32[8,128]{1,0:T(8,128)S(1)} %get-tuple-element.40.pen_ref, s32[8,128]{1,0:T(8,128)S(1)} %get-tuple-element.41.face_ref, ...), custom_call_target="tpu_custom_call" | custom-call | tf_op jit(solution)/shard_map/pallas_call | solution.py:662

commit v3 on v2

--- a/solution.py
+++ b/solution.py
@@ -31,7 +31,7 @@
 DEPTH = 12
 BATCH = 4
 OWN_BATCHES = OWN_GROUPS // BATCH
-UNROLL = 16
+PHASES = (4, 28)
 CHAINS = 4
 FORCE_UNROLL = 8
 LOOP_UNROLL = 4
@@ -155,8 +155,8 @@
 
 def prep_kernel(
     live_h, ns_h, nm_h, qw_h, sec_h, mst_h, off_h, jac_h, slot_h, face_h, rank_h,
-    x_ref, wt_ref, nq_ref, off_ref, jl_ref, slot_ref, code_ref, key_ref, over_pen, over_key, over_gap, area_ref,
-    live_s, ns_ref, nm_ref, qw_ref, jac_ref, face_ref, rank_ref, pen_ref, gap_ref, packs, accs, s_small, s_big,
+    load_ref, nq_ref, pen_ref, gap_ref, jl_ref, slot_ref, code_ref, key_ref, over_pen, over_key, over_gap, pair_ref,
+    x_ref, wt_ref, off_ref, live_s, ns_ref, nm_ref, qw_ref, jac_ref, face_ref, rank_ref, packs, accs, s_small, s_big,
 ):
     lines = slot_ref.shape[0]
     k_size, p_size = ns_ref.shape
@@ -171,34 +171,17 @@
     ]
     for copy in small:
         copy.start()
-    for base, source in ((0, sec_h), (k_size, mst_h)):
-        for at in range(0, k_size, 2 * SUB):
-            pltpu.make_async_copy(
-                source.at[at : at + 2 * SUB, :], x_ref.at[base + at : base + at + 2 * SUB, :], s_big
-            ).start(priority=1)
+    starts = [sum(PHASES[:i]) * TILE for i in range(len(PHASES))]
+    for i, tiles in enumerate(PHASES):
+        for half in range(2):
+            width = tiles * TILE // 2
+            cols = pl.ds(starts[i] + half * width, width)
+            for base, source in ((0, sec_h), (k_size, mst_h)):
+                pltpu.make_async_copy(
+                    source.at[:, cols], x_ref.at[base : base + k_size, cols], s_big.at[i]
+                ).start(priority=1)
     for copy in small:
         copy.wait()
-
-    row_id = (
-        lax.broadcasted_iota(jnp.int32, (lines, LANES), 0) * LANES
-        + lax.broadcasted_iota(jnp.int32, (lines, LANES), 1)
-    )
-    alive = row_id < live_s[...]
-    group = jnp.where(alive, slot_ref[...] // WIDTH, -1)
-    before = (
-        lax.broadcasted_iota(jnp.int32, (lines, lines), 1)
-        < lax.broadcasted_iota(jnp.int32, (lines, lines), 0)
-    )
-    before = jnp.where(before, 1.0, 0.0).astype(jnp.bfloat16)
-    place = jnp.zeros((lines, LANES), jnp.float32)
-    for g in range(0, GROUPS, 2):
-        mine = [group == g, group == g + 1]
-        seen = jnp.concatenate([jnp.where(m, 1.0, 0.0).astype(jnp.bfloat16) for m in mine], axis=1)
-        found = jnp.dot(before, seen, preferred_element_type=jnp.float32)
-        place = jnp.where(mine[0], found[:, :LANES], jnp.where(mine[1], found[:, LANES:], place))
-    code = jnp.where(alive, place.astype(jnp.int32) * CODE + group, -1)
-    code_ref[...] = code
-    worst = jnp.max(code)
 
     w = jnp.concatenate([ns_ref[...], -nm_ref[...]], axis=0).astype(jnp.float32)
     qrow = qw_ref[...]
@@ -221,26 +204,59 @@
     low = (scaled - top.astype(jnp.float32)).astype(jnp.bfloat16)
     nq_ref[...] = jnp.concatenate([top, low], axis=0)
 
+    weights = wt_ref[...]
+
+    def dense(phase):
+        done = x_ref.at[:, pl.ds(starts[phase], PHASES[phase] * TILE)]
+        pltpu.make_async_copy(done, done, s_big.at[phase]).wait()
+        for i in range(PHASES[phase]):
+            tile = starts[phase] // TILE + i
+            cols = pl.ds(tile * TILE, TILE)
+            field = project(weights, x_ref, off_ref, tile)
+            for at in range(0, p_size, 2 * SUB):
+                load_ref[at : at + 2 * SUB, cols] = jnp.minimum(field[at : at + 2 * SUB].astype(jnp.bfloat16), 0)
+            reduce_field(field, p_size, tile, pen_ref, gap_ref)
+
+    dense(0)
+    row_id = (
+        lax.broadcasted_iota(jnp.int32, (lines, LANES), 0) * LANES
+        + lax.broadcasted_iota(jnp.int32, (lines, LANES), 1)
+    )
+    alive = row_id < live_s[...]
+    group = jnp.where(alive, slot_ref[...] // WIDTH, -1)
+    before = (
+        lax.broadcasted_iota(jnp.int32, (lines, lines), 1)
+        < lax.broadcasted_iota(jnp.int32, (lines, lines), 0)
+    )
+    before = jnp.where(before, 1.0, 0.0).astype(jnp.bfloat16)
+    place = jnp.zeros((lines, LANES), jnp.float32)
+    for g in range(0, GROUPS, 2):
+        mine = [group == g, group == g + 1]
+        seen = jnp.concatenate([jnp.where(m, 1.0, 0.0).astype(jnp.bfloat16) for m in mine], axis=1)
+        found = jnp.dot(before, seen, preferred_element_type=jnp.float32)
+        place = jnp.where(mine[0], found[:, :LANES], jnp.where(mine[1], found[:, LANES:], place))
+    code = jnp.where(alive, place.astype(jnp.int32) * CODE + group, -1)
+    code_ref[...] = code
+    worst = jnp.max(code)
+
     key_ref[...] = ((rank_ref[...] - 2) << 30) + (FACE_MASK - face_ref[...])
     jl = jnp.where(alive, jac_ref[...], 0.0)
     jl_ref[...] = jl
-    area_ref[...] = jnp.sum(jl, axis=0, keepdims=True) * jnp.sum(qrow, axis=1, keepdims=True)
     over_pen[...] = jnp.full(over_pen.shape, LOWEST_FILL, jnp.float32)
     over_key[...] = jnp.full(over_key.shape, KEY_LOW, jnp.int32)
     over_gap[...] = jnp.zeros(over_gap.shape, jnp.float32)
 
-    pltpu.make_async_copy(x_ref, x_ref, s_big).wait()
+    for phase in range(1, len(PHASES)):
+        dense(phase)
+    row_gap = gap_ref[...] * jl
+    gap_ref[...] = row_gap
+    total_gap = jnp.sum(jnp.sum(row_gap, axis=0, keepdims=True), axis=1, keepdims=True)
+    total_area = jnp.sum(jnp.sum(jl, axis=0, keepdims=True), axis=1, keepdims=True)
+    total_area = total_area * jnp.sum(qrow, axis=1, keepdims=True)
+    pair_ref[...] = jnp.where(lane_row == 0, total_gap, jnp.where(lane_row == 1, total_area, 0.0))
 
     @pl.when(worst >= DEPTH * CODE)
     def _():
-        weights = wt_ref[...]
-
-        def fill(tile, carry):
-            reduce_field(project(weights, x_ref, off_ref, tile), p_size, tile, pen_ref, gap_ref)
-            return carry
-
-        lax.fori_loop(0, rows // TILE, fill, 0)
-        gap_ref[...] = gap_ref[...] * jl_ref[...]
         face_ref[...] = code_ref[...]
 
         def one(worst):
@@ -270,17 +286,16 @@
 
 def main_kernel(
     n_dom, n_rep,
-    x_ref, wt_ref, nq_ref, off_ref, jl_ref, slot_ref, code_ref, key_ref, over_pen, over_key, over_gap, area_ref,
+    load_ref, nq_ref, pen_ref, gap_ref, jl_ref, slot_ref, code_ref, key_ref, over_pen, over_key, over_gap, pair_ref,
     force_ref, out_pen, out_face, out_gap, out_mean,
-    load_ref, pen_ref, gap_ref, packs, even_accs, odd_accs, raw_pen, raw_key, raw_gap,
-    sp_sf, sp_si, ow_sf, ow_si, t1_s, t2_s, sp_f, sp_i, ow_f, ow_i, t1_d, t2_d,
+    packs, even_accs, odd_accs, raw_pen, raw_key, raw_gap,
+    sp_sf, sp_si, ow_sf, ow_si, t2_s, sp_f, sp_i, ow_f, ow_i, t1_d, t2_d,
     s_spf, r_spf, s_spi, r_spi, s_owf, r_owf, s_owi, r_owi, s_t1, r_t1, s_t2, r_t2, inside,
 ):
     dom = lax.axis_index("dom")
     rep = lax.axis_index("rep")
     k_size = force_ref.shape[0]
     rows = force_ref.shape[1]
-    p_size = load_ref.shape[0]
     per_tile = TILE // LANES
     tiles = rows // TILE
     count = n_dom * n_rep
@@ -305,50 +320,21 @@
     signal(barrier, dom * n_rep, me)
     signal(barrier, jnp.maximum(dom - 1, 0) * n_rep, dom * n_rep)
 
-    wt = wt_ref[...]
-
     def wide_row(ref, tile):
         return jnp.concatenate([row(ref, tile * per_tile + i) for i in range(per_tile)], axis=1)
 
     last_dom = dom == n_dom - 1
+    mate = rep + 1 - 2 * lax.rem(rep, 2)
+    first_copy = pltpu.make_async_remote_copy(
+        src_ref=pair_ref, dst_ref=t1_d, send_sem=s_t1, recv_sem=r_t1,
+        device_id=dev(dom, mate), device_id_type=MESH,
+    )
 
     def enter():
         after = n_rep * jnp.where(last_dom, 0, 1)
         pl.semaphore_wait(barrier, me + (n_rep - 1 - rep) + after)
         signal(inside, 0, me)
-
-    def batch(step, carry):
-        @pl.when(last_dom & (step == 1))
-        def _():
-            enter()
-
-        for i in range(UNROLL):
-            tile = step * UNROLL + i
-            cols = pl.ds(tile * TILE, TILE)
-            field = project(wt, x_ref, off_ref, tile)
-            for at in range(0, p_size, 2 * SUB):
-                load_ref[at : at + 2 * SUB, cols] = jnp.minimum(field[at : at + 2 * SUB].astype(jnp.bfloat16), 0)
-            reduce_field(field, p_size, tile, pen_ref, gap_ref)
-        return carry
-
-    lax.fori_loop(0, tiles // UNROLL, batch, 0)
-    row_gap = gap_ref[...] * jl_ref[...]
-    gap_ref[...] = row_gap
-    total_gap = jnp.sum(jnp.sum(row_gap, axis=0, keepdims=True), axis=1, keepdims=True)
-    total_area = jnp.sum(area_ref[...], axis=1, keepdims=True)
-    lane = lax.broadcasted_iota(jnp.int32, (1, LANES), 1)
-    t1_s[...] = jnp.where(lane == 0, total_gap, jnp.where(lane == 1, total_area, 0.0))
-
-    @pl.when(jnp.logical_not(last_dom))
-    def _():
-        enter()
-
-    mate = rep + 1 - 2 * lax.rem(rep, 2)
-    first_copy = pltpu.make_async_remote_copy(
-        src_ref=t1_s, dst_ref=t1_d, send_sem=s_t1, recv_sem=r_t1,
-        device_id=dev(dom, mate), device_id_type=MESH,
-    )
-    first_copy.start()
+        first_copy.start()
 
     def pull_batch(first):
         pull_groups(first, BATCH, 0, DEPTH, code_ref, (slot_ref, pen_ref, key_ref, gap_ref), packs)
@@ -374,6 +360,11 @@
         return rank, face
 
     pull_batch(OWN_GROUPS)
+
+    @pl.when(last_dom)
+    def _():
+        enter()
+
     match_pair(OWN_GROUPS, 0, even_accs, None, 0, 0)
     match_pair(OWN_GROUPS, 1, odd_accs, even_accs, OWN_ROWS, 0)
     close_pair(odd_accs, OWN_ROWS + 1, 1)
@@ -383,6 +374,10 @@
     sp_sf[SPILL_ROWS:, :] = raw_gap[part, :]
     sp_si[0:SPILL_ROWS, :] = rank
     sp_si[SPILL_ROWS:, :] = face
+
+    @pl.when(jnp.logical_not(last_dom))
+    def _():
+        enter()
 
     def spill_copy(j):
         where = dev(dom + 1, rep + j)
@@ -404,7 +399,7 @@
     first_copy.wait_recv()
     pairs = count // 2
     pair = lax.div(me, 2)
-    both = t1_s[...] + t1_d[...]
+    both = pair_ref[...] + t1_d[...]
     t2_s[...] = both
     t2_d[pl.ds(pair, 1), :] = both
 
@@ -581,9 +576,9 @@
         held = pl.pallas_call(
             prep_kernel,
             out_shape=(
-                pltpu.VMEM((2 * k_size, rows), bf16),
-                pltpu.VMEM((p_size + EXTRA, depth), bf16),
+                pltpu.VMEM((p_size, rows), bf16),
                 pltpu.VMEM((2 * k_size, p_size), bf16),
+                pltpu.VMEM((lines, LANES), f32),
                 pltpu.VMEM((lines, LANES), f32),
                 pltpu.VMEM((lines, LANES), f32),
                 pltpu.VMEM((lines, LANES), i32),
@@ -597,6 +592,9 @@
             in_specs=[anywhere] * 11,
             out_specs=(vmem,) * 12,
             scratch_shapes=[
+                pltpu.VMEM((2 * k_size, rows), bf16),
+                pltpu.VMEM((p_size + EXTRA, depth), bf16),
+                pltpu.VMEM((lines, LANES), f32),
                 pltpu.VMEM((1, 1), i32),
                 pltpu.VMEM((k_size, p_size), bf16),
                 pltpu.VMEM((k_size, p_size), bf16),
@@ -604,12 +602,10 @@
                 pltpu.VMEM((lines, LANES), f32),
                 pltpu.VMEM((lines, LANES), i32),
                 pltpu.VMEM((lines, LANES), i32),
-                pltpu.VMEM((lines, LANES), f32),
-                pltpu.VMEM((lines, LANES), f32),
                 packs(SUB),
                 lanes(),
                 dma((9,)),
-                dma,
+                dma((len(PHASES),)),
             ],
             compiler_params=pltpu.CompilerParams(vmem_limit_bytes=VMEM_LIMIT),
         )(
@@ -632,9 +628,6 @@
             in_specs=[vmem] * 12,
             out_specs=(vmem,) * 5,
             scratch_shapes=[
-                pltpu.VMEM((p_size, rows), bf16),
-                pltpu.VMEM((lines, LANES), f32),
-                pltpu.VMEM((lines, LANES), f32),
                 packs(BATCH * DEPTH),
                 lanes(),
                 lanes(),
@@ -645,7 +638,6 @@
                 pltpu.VMEM(spill, i32),
                 pltpu.VMEM(own, f32),
                 pltpu.VMEM(own, i32),
-                pltpu.VMEM((1, LANES), f32),
                 pltpu.VMEM((1, LANES), f32),
                 pltpu.VMEM((n_rep,) + spill, f32),
                 pltpu.VMEM((n_rep,) + spill, i32),

time: 17.8 us -> 18.2 us (1.022)
  Pallas kernels: 16.3 us -> 16.8 us
    pallas_call x1, Pallas kernels: 1.71 us -> 3.09 us  [shards(): pl.pallas_call(prep_kernel, out_shape=(pltpu.VMEM((p_size, rows), bf16),...]
    pallas_call x1, Pallas kernels: 12.9 us -> 12 us  [shards(): pl.pallas_call(functools.partial(main_kernel, n_dom, n_rep), out_shape=(p...]
where the time goes in v3:
time: 18.2 us; the launch traced here: 18.1 us
  Pallas kernels  16.8 us (92%)
  between operations  1.3 us (7%)
    pallas_call x1, Pallas kernels, shards(): pl.pallas_call(functools.partial(main_kernel, n_dom, n_rep), out_shape=(p...  12 us
    pallas_call x1, Pallas kernels, shards(): pl.pallas_call(prep_kernel, out_shape=(pltpu.VMEM((p_size, rows), bf16),...  3.09 us
    pallas_call x1, Pallas kernels, shards(): pl.pallas_call(finish_kernel, out_shape=tuple((jax.ShapeDtypeStruct(x.sha...  1.64 us

profile of v3, /device:TPU:0, one launch (start us, length us, event | category | flops | bytes accessed | tf_op | source)
XLA Modules:
  0.0 18.1 jit_solution(13274704380205497428)
XLA Ops:
  1.3 3.1 %shard_map.146 = (bf16[256,8192]{1,0:T(8,128)(2,1)S(1)}, bf16[128,256]{1,0:T(8,128)(2,1)S(1)}, f32[64,128]{1,0:T(8,128)S(1)}, f32[64,128]{1,0:T(8,128)S(1)}, f32...) custom-call(s32[1,1]{1,0:T(1,128)} %bitcast.11.live_h, ...), custom_call_target="tpu_custom_call" | custom-call | tf_op jit(solution)/shard_map/pallas_call | solution.py:576
  4.4 12.0 %shard_map.147 = (bf16[64,8192]{1,0:T(8,128)(2,1)S(1)}, f32[8,128]{1,0:T(8,128)S(1)}, s32[8,128]{1,0:T(8,128)S(1)}, f32[8,128]{1,0:T(8,128)S(1)}, f32[1,1]{1,0:T(1,128)}) custom-call(bf16[256,8192]{1,0:T(8,128)(2,1)S(1)} %get-tuple-element.27.load_ref, bf16[128,256]{1,0:T(8,128)(2,1)S(1)} %get-tuple-element.28.nq_ref, ...), custom_call_target="tpu_custom_call" | custom-call | tf_op jit(solution)/shard_map/pallas_call | solution.py:619
  16.4 1.6 %shard_map.148 = (bf16[64,8192]{1,0:T(8,128)(2,1)}, f32[8,128]{1,0:T(8,128)}, s32[8,128]{1,0:T(8,128)}, f32[8,128]{1,0:T(8,128)}, f32[1,1]{1,0:T(1,128)}) custom-call(bf16[64,8192]{1,0:T(8,128)(2,1)S(1)} %get-tuple-element.39.force_ref, f32[8,128]{1,0:T(8,128)S(1)} %get-tuple-element.40.pen_ref, s32[8,128]{1,0:T(8,128)S(1)} %get-tuple-element.41.face_ref, ...), custom_call_target="tpu_custom_call" | custom-call | tf_op jit(solution)/shard_map/pallas_call | solution.py:654

commit v4 on v3

--- a/solution.py
+++ b/solution.py
@@ -26,7 +26,7 @@
 FACE_LIMIT = 1073741824
 FACE_MASK = FACE_LIMIT - 1
 KEY_LOW = -2147483648
-MESH = pl.DeviceIdType.MESH
+LOGICAL = pl.DeviceIdType.LOGICAL
 TILE = 256
 DEPTH = 12
 BATCH = 4
@@ -290,7 +290,7 @@
     force_ref, out_pen, out_face, out_gap, out_mean,
     packs, even_accs, odd_accs, raw_pen, raw_key, raw_gap,
     sp_sf, sp_si, ow_sf, ow_si, t2_s, sp_f, sp_i, ow_f, ow_i, t1_d, t2_d,
-    s_spf, r_spf, s_spi, r_spi, s_owf, r_owf, s_owi, r_owi, s_t1, r_t1, s_t2, r_t2, inside,
+    s_spf, r_spf, s_spi, r_spi, s_owf, r_owf, s_owi, r_owi, s_t1, r_t1, s_t2, r_t2, inside, follows,
 ):
     dom = lax.axis_index("dom")
     rep = lax.axis_index("rep")
@@ -301,40 +301,34 @@
     count = n_dom * n_rep
     me = dom * n_rep + rep
 
-    def dev(d, r):
-        return {"dom": lax.rem(d + n_dom, n_dom), "rep": lax.rem(r + n_rep, n_rep)}
-
-    def flat_dev(flat):
-        return dev(lax.div(flat, n_rep), lax.rem(flat, n_rep))
+    def flat(d, r):
+        return lax.rem(d + n_dom, n_dom) * n_rep + lax.rem(r + n_rep, n_rep)
 
     barrier = pltpu.get_barrier_semaphore()
 
     def signal(sem, first, last):
-        def one(flat, carry):
-            pl.semaphore_signal(sem, inc=1, device_id=flat_dev(flat), device_id_type=MESH)
+        def one(other, carry):
+            pl.semaphore_signal(sem, inc=1, device_id=other, device_id_type=LOGICAL)
             return carry
 
         lax.fori_loop(first, last, one, 0)
 
+    odd = lax.rem(rep, 2)
+    mate = rep + 1 - 2 * odd
     signal(barrier, me + 1, count)
-    signal(barrier, dom * n_rep, me)
-    signal(barrier, jnp.maximum(dom - 1, 0) * n_rep, dom * n_rep)
+    signal(barrier, me - odd, me)
 
     def wide_row(ref, tile):
         return jnp.concatenate([row(ref, tile * per_tile + i) for i in range(per_tile)], axis=1)
 
     last_dom = dom == n_dom - 1
-    mate = rep + 1 - 2 * lax.rem(rep, 2)
     first_copy = pltpu.make_async_remote_copy(
         src_ref=pair_ref, dst_ref=t1_d, send_sem=s_t1, recv_sem=r_t1,
-        device_id=dev(dom, mate), device_id_type=MESH,
-    )
-
-    def enter():
-        after = n_rep * jnp.where(last_dom, 0, 1)
-        pl.semaphore_wait(barrier, me + (n_rep - 1 - rep) + after)
-        signal(inside, 0, me)
-        first_copy.start()
+        device_id=flat(dom, mate), device_id_type=LOGICAL,
+    )
+    pl.semaphore_wait(barrier, me + 1 - odd)
+    first_copy.start()
+    signal(follows, jnp.maximum(dom - 1, 0) * n_rep, dom * n_rep)
 
     def pull_batch(first):
         pull_groups(first, BATCH, 0, DEPTH, code_ref, (slot_ref, pen_ref, key_ref, gap_ref), packs)
@@ -360,10 +354,6 @@
         return rank, face
 
     pull_batch(OWN_GROUPS)
-
-    @pl.when(last_dom)
-    def _():
-        enter()
 
     match_pair(OWN_GROUPS, 0, even_accs, None, 0, 0)
     match_pair(OWN_GROUPS, 1, odd_accs, even_accs, OWN_ROWS, 0)
@@ -377,18 +367,18 @@
 
     @pl.when(jnp.logical_not(last_dom))
     def _():
-        enter()
+        pl.semaphore_wait(follows, n_rep)
 
     def spill_copy(j):
-        where = dev(dom + 1, rep + j)
+        where = flat(dom + 1, rep + j)
         return (
             pltpu.make_async_remote_copy(
                 src_ref=sp_sf, dst_ref=sp_f.at[rep], send_sem=s_spf, recv_sem=r_spf,
-                device_id=where, device_id_type=MESH,
+                device_id=where, device_id_type=LOGICAL,
             ),
             pltpu.make_async_remote_copy(
                 src_ref=sp_si, dst_ref=sp_i.at[rep], send_sem=s_spi, recv_sem=r_spi,
-                device_id=where, device_id_type=MESH,
+                device_id=where, device_id_type=LOGICAL,
             ),
         )
 
@@ -396,6 +386,7 @@
         for copy in spill_copy(j):
             copy.start()
 
+    signal(inside, 0, me)
     first_copy.wait_recv()
     pairs = count // 2
     pair = lax.div(me, 2)
@@ -407,7 +398,7 @@
         def one(other, carry):
             pltpu.make_async_remote_copy(
                 src_ref=t2_s, dst_ref=t2_d.at[pl.ds(pair, 1), :], send_sem=s_t2, recv_sem=r_t2,
-                device_id=flat_dev(other * 2 + lax.rem(rep, 2)), device_id_type=MESH,
+                device_id=other * 2 + odd, device_id_type=LOGICAL,
             ).start()
             return carry
 
@@ -423,7 +414,7 @@
         send_pairs(pair + 1, pairs)
 
     quarter = lax.div(me * 4, count)
-    turn = OWN_BATCHES - quarter - jnp.where(quarter >= 2, 1, 0)
+    turn = OWN_BATCHES - jnp.maximum(quarter * 2 - 3, 0)
 
     def own_scan(i, carry):
         @pl.when(i == turn)
@@ -439,6 +430,10 @@
 
     lax.fori_loop(0, OWN_BATCHES, own_scan, 0)
     close_pair(odd_accs, OWN_ROWS - 1, OWN_ROWS - 1)
+    @pl.when(turn >= OWN_BATCHES)
+    def _():
+        send_up()
+
     rank, face = decode(raw_pen[...], raw_key[...])
     ow_sf[0] = raw_pen[...]
     ow_sf[1] = raw_gap[...]
@@ -446,15 +441,15 @@
     ow_si[1] = face
 
     def own_copy(j):
-        where = dev(dom, rep + j)
+        where = flat(dom, rep + j)
         return (
             pltpu.make_async_remote_copy(
                 src_ref=ow_sf, dst_ref=ow_f.at[rep], send_sem=s_owf, recv_sem=r_owf,
-                device_id=where, device_id_type=MESH,
+                device_id=where, device_id_type=LOGICAL,
             ),
             pltpu.make_async_remote_copy(
                 src_ref=ow_si, dst_ref=ow_i.at[rep], send_sem=s_owi, recv_sem=r_owi,
-                device_id=where, device_id_type=MESH,
+                device_id=where, device_id_type=LOGICAL,
             ),
         )
 
@@ -463,10 +458,6 @@
             copy.start()
     ow_f[rep] = ow_sf[...]
     ow_i[rep] = ow_si[...]
-
-    @pl.when(turn >= OWN_BATCHES)
-    def _():
-        send_up()
 
     nq = nq_ref[...]
 
@@ -645,7 +636,7 @@
                 pltpu.VMEM((n_rep,) + own, i32),
                 pltpu.VMEM((1, LANES), f32),
                 pltpu.VMEM((pairs, LANES), f32),
-            ] + [dma] * 12 + [pltpu.SemaphoreType.REGULAR],
+            ] + [dma] * 12 + [pltpu.SemaphoreType.REGULAR] * 2,
             compiler_params=pltpu.CompilerParams(
                 collective_id=0, has_side_effects=True, vmem_limit_bytes=VMEM_LIMIT
             ),

time: 18.2 us -> 19.1 us (1.049)
  Pallas kernels: 16.8 us -> 17.7 us
    pallas_call x1, Pallas kernels: 12 us -> 12.9 us  [shards(): pl.pallas_call(functools.partial(main_kernel, n_dom, n_rep), out_shape=(p...]
where the time goes in v4:
time: 19.1 us; the launch traced here: 19 us
  Pallas kernels  17.7 us (93%)
  between operations  1.3 us (7%)
    pallas_call x1, Pallas kernels, shards(): pl.pallas_call(functools.partial(main_kernel, n_dom, n_rep), out_shape=(p...  12.9 us
    pallas_call x1, Pallas kernels, shards(): pl.pallas_call(prep_kernel, out_shape=(pltpu.VMEM((p_size, rows), bf16),...  3.09 us
    pallas_call x1, Pallas kernels, shards(): pl.pallas_call(finish_kernel, out_shape=tuple((jax.ShapeDtypeStruct(x.sha...  1.64 us

profile of v4, /device:TPU:0, one launch (start us, length us, event | category | flops | bytes accessed | tf_op | source)
XLA Modules:
  0.0 19.0 jit_solution(11238952836191340043)
XLA Ops:
  1.3 3.1 %shard_map.146 = (bf16[256,8192]{1,0:T(8,128)(2,1)S(1)}, bf16[128,256]{1,0:T(8,128)(2,1)S(1)}, f32[64,128]{1,0:T(8,128)S(1)}, f32[64,128]{1,0:T(8,128)S(1)}, f32...) custom-call(s32[1,1]{1,0:T(1,128)} %bitcast.11.live_h, ...), custom_call_target="tpu_custom_call" | custom-call | tf_op jit(solution)/shard_map/pallas_call | solution.py:567
  4.4 12.9 %shard_map.147 = (bf16[64,8192]{1,0:T(8,128)(2,1)S(1)}, f32[8,128]{1,0:T(8,128)S(1)}, s32[8,128]{1,0:T(8,128)S(1)}, f32[8,128]{1,0:T(8,128)S(1)}, f32[1,1]{1,0:T(1,128)}) custom-call(bf16[256,8192]{1,0:T(8,128)(2,1)S(1)} %get-tuple-element.27.load_ref, bf16[128,256]{1,0:T(8,128)(2,1)S(1)} %get-tuple-element.28.nq_ref, ...), custom_call_target="tpu_custom_call" | custom-call | tf_op jit(solution)/shard_map/pallas_call | solution.py:610
  17.3 1.6 %shard_map.148 = (bf16[64,8192]{1,0:T(8,128)(2,1)}, f32[8,128]{1,0:T(8,128)}, s32[8,128]{1,0:T(8,128)}, f32[8,128]{1,0:T(8,128)}, f32[1,1]{1,0:T(1,128)}) custom-call(bf16[64,8192]{1,0:T(8,128)(2,1)S(1)} %get-tuple-element.39.force_ref, f32[8,128]{1,0:T(8,128)S(1)} %get-tuple-element.40.pen_ref, s32[8,128]{1,0:T(8,128)S(1)} %get-tuple-element.41.face_ref, ...), custom_call_target="tpu_custom_call" | custom-call | tf_op jit(solution)/shard_map/pallas_call | solution.py:645

commit v5 on v4

--- a/solution.py
+++ b/solution.py
@@ -290,7 +290,7 @@
     force_ref, out_pen, out_face, out_gap, out_mean,
     packs, even_accs, odd_accs, raw_pen, raw_key, raw_gap,
     sp_sf, sp_si, ow_sf, ow_si, t2_s, sp_f, sp_i, ow_f, ow_i, t1_d, t2_d,
-    s_spf, r_spf, s_spi, r_spi, s_owf, r_owf, s_owi, r_owi, s_t1, r_t1, s_t2, r_t2, inside, follows,
+    s_spf, r_spf, s_spi, r_spi, s_owf, r_owf, s_owi, r_owi, s_t1, r_t1, s_t2, r_t2, inside, follows, peers,
 ):
     dom = lax.axis_index("dom")
     rep = lax.axis_index("rep")
@@ -306,9 +306,9 @@
 
     barrier = pltpu.get_barrier_semaphore()
 
-    def signal(sem, first, last):
-        def one(other, carry):
-            pl.semaphore_signal(sem, inc=1, device_id=other, device_id_type=LOGICAL)
+    def signal(sem, first, last, step=1, at=0):
+        def one(i, carry):
+            pl.semaphore_signal(sem, inc=1, device_id=i * step + at, device_id_type=LOGICAL)
             return carry
 
         lax.fori_loop(first, last, one, 0)
@@ -328,7 +328,11 @@
     )
     pl.semaphore_wait(barrier, me + 1 - odd)
     first_copy.start()
+    pairs = count // 2
+    pair = lax.div(me, 2)
+    signal(inside, 0, pair, 2, odd)
     signal(follows, jnp.maximum(dom - 1, 0) * n_rep, dom * n_rep)
+    signal(peers, dom * n_rep, me)
 
     def pull_batch(first):
         pull_groups(first, BATCH, 0, DEPTH, code_ref, (slot_ref, pen_ref, key_ref, gap_ref), packs)
@@ -386,10 +390,7 @@
         for copy in spill_copy(j):
             copy.start()
 
-    signal(inside, 0, me)
     first_copy.wait_recv()
-    pairs = count // 2
-    pair = lax.div(me, 2)
     both = pair_ref[...] + t1_d[...]
     t2_s[...] = both
     t2_d[pl.ds(pair, 1), :] = both
@@ -407,9 +408,9 @@
     send_pairs(0, pair)
 
     def send_up():
-        @pl.when(me < count - 1)
+        @pl.when(pair < pairs - 1)
         def _():
-            pl.semaphore_wait(inside, count - 1 - me)
+            pl.semaphore_wait(inside, pairs - 1 - pair)
 
         send_pairs(pair + 1, pairs)
 
@@ -430,15 +431,15 @@
 
     lax.fori_loop(0, OWN_BATCHES, own_scan, 0)
     close_pair(odd_accs, OWN_ROWS - 1, OWN_ROWS - 1)
-    @pl.when(turn >= OWN_BATCHES)
-    def _():
-        send_up()
-
     rank, face = decode(raw_pen[...], raw_key[...])
     ow_sf[0] = raw_pen[...]
     ow_sf[1] = raw_gap[...]
     ow_si[0] = rank
     ow_si[1] = face
+
+    @pl.when(rep < n_rep - 1)
+    def _():
+        pl.semaphore_wait(peers, n_rep - 1 - rep)
 
     def own_copy(j):
         where = flat(dom, rep + j)
@@ -458,6 +459,10 @@
             copy.start()
     ow_f[rep] = ow_sf[...]
     ow_i[rep] = ow_si[...]
+
+    @pl.when(turn >= OWN_BATCHES)
+    def _():
+        send_up()
 
     nq = nq_ref[...]
 
@@ -636,7 +641,7 @@
                 pltpu.VMEM((n_rep,) + own, i32),
                 pltpu.VMEM((1, LANES), f32),
                 pltpu.VMEM((pairs, LANES), f32),
-            ] + [dma] * 12 + [pltpu.SemaphoreType.REGULAR] * 2,
+            ] + [dma] * 12 + [pltpu.SemaphoreType.REGULAR] * 3,
             compiler_params=pltpu.CompilerParams(
                 collective_id=0, has_side_effects=True, vmem_limit_bytes=VMEM_LIMIT
             ),

time: 19.1 us -> 18.5 us (0.969)
  Pallas kernels: 17.7 us -> 17 us
    pallas_call x1, Pallas kernels: 12.9 us -> 12.2 us  [shards(): pl.pallas_call(functools.partial(main_kernel, n_dom, n_rep), out_shape=(p...]
where the time goes in v5:
time: 18.5 us; the launch traced here: 18.3 us
  Pallas kernels  17 us (92%)
  between operations  1.3 us (7%)
    pallas_call x1, Pallas kernels, shards(): pl.pallas_call(functools.partial(main_kernel, n_dom, n_rep), out_shape=(p...  12.2 us
    pallas_call x1, Pallas kernels, shards(): pl.pallas_call(prep_kernel, out_shape=(pltpu.VMEM((p_size, rows), bf16),...  3.09 us
    pallas_call x1, Pallas kernels, shards(): pl.pallas_call(finish_kernel, out_shape=tuple((jax.ShapeDtypeStruct(x.sha...  1.64 us

profile of v5, /device:TPU:0, one launch (start us, length us, event | category | flops | bytes accessed | tf_op | source)
XLA Modules:
  0.0 18.3 jit_solution(1876743055168580557)
XLA Ops:
  1.3 3.1 %shard_map.146 = (bf16[256,8192]{1,0:T(8,128)(2,1)S(1)}, bf16[128,256]{1,0:T(8,128)(2,1)S(1)}, f32[64,128]{1,0:T(8,128)S(1)}, f32[64,128]{1,0:T(8,128)S(1)}, f32...) custom-call(s32[1,1]{1,0:T(1,128)} %bitcast.11.live_h, ...), custom_call_target="tpu_custom_call" | custom-call | tf_op jit(solution)/shard_map/pallas_call | solution.py:572
  4.4 12.2 %shard_map.147 = (bf16[64,8192]{1,0:T(8,128)(2,1)S(1)}, f32[8,128]{1,0:T(8,128)S(1)}, s32[8,128]{1,0:T(8,128)S(1)}, f32[8,128]{1,0:T(8,128)S(1)}, f32[1,1]{1,0:T(1,128)}) custom-call(bf16[256,8192]{1,0:T(8,128)(2,1)S(1)} %get-tuple-element.27.load_ref, bf16[128,256]{1,0:T(8,128)(2,1)S(1)} %get-tuple-element.28.nq_ref, ...), custom_call_target="tpu_custom_call" | custom-call | tf_op jit(solution)/shard_map/pallas_call | solution.py:615
  16.6 1.6 %shard_map.148 = (bf16[64,8192]{1,0:T(8,128)(2,1)}, f32[8,128]{1,0:T(8,128)}, s32[8,128]{1,0:T(8,128)}, f32[8,128]{1,0:T(8,128)}, f32[1,1]{1,0:T(1,128)}) custom-call(bf16[64,8192]{1,0:T(8,128)(2,1)S(1)} %get-tuple-element.39.force_ref, f32[8,128]{1,0:T(8,128)S(1)} %get-tuple-element.40.pen_ref, s32[8,128]{1,0:T(8,128)S(1)} %get-tuple-element.41.face_ref, ...), custom_call_target="tpu_custom_call" | custom-call | tf_op jit(solution)/shard_map/pallas_call | solution.py:650

commit v6 on v2

--- a/solution.py
+++ b/solution.py
@@ -26,7 +26,7 @@
 FACE_LIMIT = 1073741824
 FACE_MASK = FACE_LIMIT - 1
 KEY_LOW = -2147483648
-MESH = pl.DeviceIdType.MESH
+LOGICAL = pl.DeviceIdType.LOGICAL
 TILE = 256
 DEPTH = 12
 BATCH = 4
@@ -234,21 +234,21 @@
     @pl.when(worst >= DEPTH * CODE)
     def _():
         weights = wt_ref[...]
-
-        def fill(tile, carry):
+        work = face_ref
+        line_id = lax.broadcasted_iota(jnp.int32, (lines, LANES), 0)
+        work[...] = jnp.where(code >= DEPTH * CODE, line_id * CODE + (code & (CODE - 1)), -1)
+
+        def one(mark):
+            line, g = mark // CODE, mark & (CODE - 1)
+            tile = line // (TILE // LANES)
             reduce_field(project(weights, x_ref, off_ref, tile), p_size, tile, pen_ref, gap_ref)
-            return carry
-
-        lax.fori_loop(0, rows // TILE, fill, 0)
-        gap_ref[...] = gap_ref[...] * jl_ref[...]
-        face_ref[...] = code_ref[...]
-
-        def one(worst):
-            code = face_ref[...]
-            g = worst & (CODE - 1)
-            low = jnp.maximum((worst // CODE) & -SUB, DEPTH)
-            pull_groups(g, 1, low, SUB, face_ref, (slot_ref, pen_ref, key_ref, gap_ref), packs)
-            found = match_group(g, 0, SUB, packs, 2)
+            here = row(work, line) == mark
+            values = (
+                row(slot_ref, line), row(pen_ref, line), row(key_ref, line), row(gap_ref, line) * row(jl_ref, line)
+            )
+            for ref, value in zip(packs, values):
+                ref[0:SUB, :] = jnp.where(here, value, -1) if ref is packs[0] else value
+            found = match_group(g, 0, 1, packs, 1)
             odd = jnp.full((SUB, LANES), g & 1, jnp.int32)
             for side in range(PER_ROW):
                 keep_group(accs, side, [
@@ -260,12 +260,11 @@
             over_pen[at, :] = jnp.maximum(over_pen[at, :], pen)
             over_key[at, :] = jnp.maximum(over_key[at, :], key)
             over_gap[at, :] = over_gap[at, :] + gap
-            done = ((code & (CODE - 1)) == g) & (code >= low * CODE)
-            code = jnp.where(done, -1, code)
-            face_ref[...] = code
-            return jnp.max(code)
-
-        lax.while_loop(lambda worst: worst >= DEPTH * CODE, one, worst)
+            left = jnp.where(work[...] == mark, -1, work[...])
+            work[...] = left
+            return jnp.max(left)
+
+        lax.while_loop(lambda mark: mark >= 0, one, jnp.max(work[...]))
 
 
 def main_kernel(
@@ -286,17 +285,14 @@
     count = n_dom * n_rep
     me = dom * n_rep + rep
 
-    def dev(d, r):
-        return {"dom": lax.rem(d + n_dom, n_dom), "rep": lax.rem(r + n_rep, n_rep)}
-
-    def flat_dev(flat):
-        return dev(lax.div(flat, n_rep), lax.rem(flat, n_rep))
+    def flat(d, r):
+        return lax.rem(d + n_dom, n_dom) * n_rep + lax.rem(r + n_rep, n_rep)
 
     barrier = pltpu.get_barrier_semaphore()
 
-    def signal(sem, first, last):
-        def one(flat, carry):
-            pl.semaphore_signal(sem, inc=1, device_id=flat_dev(flat), device_id_type=MESH)
+    def signal(sem, first, last, step=1, at=0):
+        def one(i, carry):
+            pl.semaphore_signal(sem, inc=1, device_id=i * step + at, device_id_type=LOGICAL)
             return carry
 
         lax.fori_loop(first, last, one, 0)
@@ -311,11 +307,15 @@
         return jnp.concatenate([row(ref, tile * per_tile + i) for i in range(per_tile)], axis=1)
 
     last_dom = dom == n_dom - 1
+    pairs = count // 2
+    pair = lax.div(me, 2)
+    odd = lax.rem(rep, 2)
+    mate = rep + 1 - 2 * odd
 
     def enter():
         after = n_rep * jnp.where(last_dom, 0, 1)
         pl.semaphore_wait(barrier, me + (n_rep - 1 - rep) + after)
-        signal(inside, 0, me)
+        signal(inside, 0, pair, 2, odd)
 
     def batch(step, carry):
         @pl.when(last_dom & (step == 1))
@@ -343,10 +343,9 @@
     def _():
         enter()
 
-    mate = rep + 1 - 2 * lax.rem(rep, 2)
     first_copy = pltpu.make_async_remote_copy(
         src_ref=t1_s, dst_ref=t1_d, send_sem=s_t1, recv_sem=r_t1,
-        device_id=dev(dom, mate), device_id_type=MESH,
+        device_id=flat(dom, mate), device_id_type=LOGICAL,
     )
     first_copy.start()
 
@@ -385,15 +384,15 @@
     sp_si[SPILL_ROWS:, :] = face
 
     def spill_copy(j):
-        where = dev(dom + 1, rep + j)
+        where = flat(dom + 1, rep + j)
         return (
             pltpu.make_async_remote_copy(
                 src_ref=sp_sf, dst_ref=sp_f.at[rep], send_sem=s_spf, recv_sem=r_spf,
-                device_id=where, device_id_type=MESH,
+                device_id=where, device_id_type=LOGICAL,
             ),
             pltpu.make_async_remote_copy(
                 src_ref=sp_si, dst_ref=sp_i.at[rep], send_sem=s_spi, recv_sem=r_spi,
-                device_id=where, device_id_type=MESH,
+                device_id=where, device_id_type=LOGICAL,
             ),
         )
 
@@ -402,8 +401,6 @@
             copy.start()
 
     first_copy.wait_recv()
-    pairs = count // 2
-    pair = lax.div(me, 2)
     both = t1_s[...] + t1_d[...]
     t2_s[...] = both
     t2_d[pl.ds(pair, 1), :] = both
@@ -412,7 +409,7 @@
         def one(other, carry):
             pltpu.make_async_remote_copy(
                 src_ref=t2_s, dst_ref=t2_d.at[pl.ds(pair, 1), :], send_sem=s_t2, recv_sem=r_t2,
-                device_id=flat_dev(other * 2 + lax.rem(rep, 2)), device_id_type=MESH,
+                device_id=other * 2 + odd, device_id_type=LOGICAL,
             ).start()
             return carry
 
@@ -421,9 +418,9 @@
     send_pairs(0, pair)
 
     def send_up():
-        @pl.when(me < count - 1)
+        @pl.when(pair < pairs - 1)
         def _():
-            pl.semaphore_wait(inside, count - 1 - me)
+            pl.semaphore_wait(inside, pairs - 1 - pair)
 
         send_pairs(pair + 1, pairs)
 
@@ -451,15 +448,15 @@
     ow_si[1] = face
 
     def own_copy(j):
-        where = dev(dom, rep + j)
+        where = flat(dom, rep + j)
         return (
             pltpu.make_async_remote_copy(
                 src_ref=ow_sf, dst_ref=ow_f.at[rep], send_sem=s_owf, recv_sem=r_owf,
-                device_id=where, device_id_type=MESH,
+                device_id=where, device_id_type=LOGICAL,
             ),
             pltpu.make_async_remote_copy(
                 src_ref=ow_si, dst_ref=ow_i.at[rep], send_sem=s_owi, recv_sem=r_owi,
-                device_id=where, device_id_type=MESH,
+                device_id=where, device_id_type=LOGICAL,
             ),
         )
 
@@ -509,11 +506,11 @@
     settle(t2_d.at[pl.ds(0, pairs - 1), :], s_t2)
 
     settle(t2_d.at[pl.ds(0, pairs - 1), :], r_t2)
+    settle(sp_f, r_spf)
+    settle(sp_i, r_spi)
     whole = jnp.sum(t2_d[...], axis=0, keepdims=True)
     out_mean[...] = whole[:, 0:1] / whole[:, 1:2]
 
-    settle(sp_f, r_spf)
-    settle(sp_i, r_spi)
     g = SPILL_ROWS
     pen_s, gap_s = sp_f[0, 0:g], sp_f[0, g:]
     key_s = encode(sp_i[0, 0:g], sp_i[0, g:])

time: 17.8 us -> 17.4 us (0.978)
  Pallas kernels: 16.3 us -> 15.9 us
    pallas_call x1, Pallas kernels: 12.9 us -> 12.6 us  [shards(): pl.pallas_call(functools.partial(main_kernel, n_dom, n_rep), out_shape=(p...]
where the time goes in v6:
time: 17.4 us; the launch traced here: 17.2 us
  Pallas kernels  15.9 us (91%)
  between operations  1.3 us (7%)
    pallas_call x1, Pallas kernels, shards(): pl.pallas_call(functools.partial(main_kernel, n_dom, n_rep), out_shape=(p...  12.6 us
    pallas_call x1, Pallas kernels, shards(): pl.pallas_call(prep_kernel, out_shape=(pltpu.VMEM((2 * k_size, rows), bf1...  1.71 us
    pallas_call x1, Pallas kernels, shards(): pl.pallas_call(finish_kernel, out_shape=tuple((jax.ShapeDtypeStruct(x.sha...  1.64 us

profile of v6, /device:TPU:0, one launch (start us, length us, event | category | flops | bytes accessed | tf_op | source)
XLA Modules:
  0.0 17.2 jit_solution(10339247782808627426)
XLA Ops:
  1.3 1.7 %shard_map.146 = (bf16[128,8192]{1,0:T(8,128)(2,1)S(1)}, bf16[272,144]{1,0:T(8,128)(2,1)S(1)}, bf16[128,256]{1,0:T(8,128)(2,1)S(1)}, f32[64,128]{1,0:T(8,128)S(1...) custom-call(s32[1,1]{1,0:T(1,128)} %bitcast.11.live_h, ...), custom_call_target="tpu_custom_call" | custom-call | tf_op jit(solution)/shard_map/pallas_call | solution.py:578
  3.0 12.6 %shard_map.147 = (bf16[64,8192]{1,0:T(8,128)(2,1)S(1)}, f32[8,128]{1,0:T(8,128)S(1)}, s32[8,128]{1,0:T(8,128)S(1)}, f32[8,128]{1,0:T(8,128)S(1)}, f32[1,1]{1,0:T(1,128)}) custom-call(bf16[128,8192]{1,0:T(8,128)(2,1)S(1)} %get-tuple-element.27.x_ref, bf16[272,144]{1,0:T(8,128)(2,1)S(1)} %get-tuple-element.28.wt_ref, ...), custom_call_target="tpu_custom_call" | custom-call | tf_op jit(solution)/shard_map/pallas_call | solution.py:620
  15.6 1.6 %shard_map.148 = (bf16[64,8192]{1,0:T(8,128)(2,1)}, f32[8,128]{1,0:T(8,128)}, s32[8,128]{1,0:T(8,128)}, f32[8,128]{1,0:T(8,128)}, f32[1,1]{1,0:T(1,128)}) custom-call(bf16[64,8192]{1,0:T(8,128)(2,1)S(1)} %get-tuple-element.39.force_ref, f32[8,128]{1,0:T(8,128)S(1)} %get-tuple-element.40.pen_ref, s32[8,128]{1,0:T(8,128)S(1)} %get-tuple-element.41.face_ref, ...), custom_call_target="tpu_custom_call" | custom-call | tf_op jit(solution)/shard_map/pallas_call | solution.py:659

commit v7 on v6

--- a/solution.py
+++ b/solution.py
@@ -31,7 +31,7 @@
 DEPTH = 12
 BATCH = 4
 OWN_BATCHES = OWN_GROUPS // BATCH
-UNROLL = 16
+UNROLL = 32
 CHAINS = 4
 FORCE_UNROLL = 8
 LOOP_UNROLL = 4
@@ -306,22 +306,12 @@
     def wide_row(ref, tile):
         return jnp.concatenate([row(ref, tile * per_tile + i) for i in range(per_tile)], axis=1)
 
-    last_dom = dom == n_dom - 1
     pairs = count // 2
     pair = lax.div(me, 2)
     odd = lax.rem(rep, 2)
     mate = rep + 1 - 2 * odd
 
-    def enter():
-        after = n_rep * jnp.where(last_dom, 0, 1)
-        pl.semaphore_wait(barrier, me + (n_rep - 1 - rep) + after)
-        signal(inside, 0, pair, 2, odd)
-
     def batch(step, carry):
-        @pl.when(last_dom & (step == 1))
-        def _():
-            enter()
-
         for i in range(UNROLL):
             tile = step * UNROLL + i
             cols = pl.ds(tile * TILE, TILE)
@@ -339,15 +329,14 @@
     lane = lax.broadcasted_iota(jnp.int32, (1, LANES), 1)
     t1_s[...] = jnp.where(lane == 0, total_gap, jnp.where(lane == 1, total_area, 0.0))
 
-    @pl.when(jnp.logical_not(last_dom))
-    def _():
-        enter()
-
+    after = n_rep * jnp.where(dom == n_dom - 1, 0, 1)
+    pl.semaphore_wait(barrier, me + (n_rep - 1 - rep) + after)
     first_copy = pltpu.make_async_remote_copy(
         src_ref=t1_s, dst_ref=t1_d, send_sem=s_t1, recv_sem=r_t1,
         device_id=flat(dom, mate), device_id_type=LOGICAL,
     )
     first_copy.start()
+    signal(inside, 0, pair, 2, odd)
 
     def pull_batch(first):
         pull_groups(first, BATCH, 0, DEPTH, code_ref, (slot_ref, pen_ref, key_ref, gap_ref), packs)

time: 17.4 us -> 16.9 us (0.971)
  Pallas kernels: 15.9 us -> 15.4 us
    pallas_call x1, Pallas kernels: 12.6 us -> 12.1 us  [shards(): pl.pallas_call(functools.partial(main_kernel, n_dom, n_rep), out_shape=(p...]
where the time goes in v7:
time: 16.9 us; the launch traced here: 16.7 us
  Pallas kernels  15.4 us (91%)
  between operations  1.3 us (8%)
    pallas_call x1, Pallas kernels, shards(): pl.pallas_call(functools.partial(main_kernel, n_dom, n_rep), out_shape=(p...  12.1 us
    pallas_call x1, Pallas kernels, shards(): pl.pallas_call(prep_kernel, out_shape=(pltpu.VMEM((2 * k_size, rows), bf1...  1.71 us
    pallas_call x1, Pallas kernels, shards(): pl.pallas_call(finish_kernel, out_shape=tuple((jax.ShapeDtypeStruct(x.sha...  1.64 us

profile of v7, /device:TPU:0, one launch (start us, length us, event | category | flops | bytes accessed | tf_op | source)
XLA Modules:
  0.0 16.7 jit_solution(11021317878842391959)
XLA Ops:
  1.3 1.7 %shard_map.146 = (bf16[128,8192]{1,0:T(8,128)(2,1)S(1)}, bf16[272,144]{1,0:T(8,128)(2,1)S(1)}, bf16[128,256]{1,0:T(8,128)(2,1)S(1)}, f32[64,128]{1,0:T(8,128)S(1...) custom-call(s32[1,1]{1,0:T(1,128)} %bitcast.11.live_h, ...), custom_call_target="tpu_custom_call" | custom-call | tf_op jit(solution)/shard_map/pallas_call | solution.py:567
  3.0 12.1 %shard_map.147 = (bf16[64,8192]{1,0:T(8,128)(2,1)S(1)}, f32[8,128]{1,0:T(8,128)S(1)}, s32[8,128]{1,0:T(8,128)S(1)}, f32[8,128]{1,0:T(8,128)S(1)}, f32[1,1]{1,0:T(1,128)}) custom-call(bf16[128,8192]{1,0:T(8,128)(2,1)S(1)} %get-tuple-element.27.x_ref, bf16[272,144]{1,0:T(8,128)(2,1)S(1)} %get-tuple-element.28.wt_ref, ...), custom_call_target="tpu_custom_call" | custom-call | tf_op jit(solution)/shard_map/pallas_call | solution.py:609
  15.1 1.6 %shard_map.148 = (bf16[64,8192]{1,0:T(8,128)(2,1)}, f32[8,128]{1,0:T(8,128)}, s32[8,128]{1,0:T(8,128)}, f32[8,128]{1,0:T(8,128)}, f32[1,1]{1,0:T(1,128)}) custom-call(bf16[64,8192]{1,0:T(8,128)(2,1)S(1)} %get-tuple-element.39.force_ref, f32[8,128]{1,0:T(8,128)S(1)} %get-tuple-element.40.pen_ref, s32[8,128]{1,0:T(8,128)S(1)} %get-tuple-element.41.face_ref, ...), custom_call_target="tpu_custom_call" | custom-call | tf_op jit(solution)/shard_map/pallas_call | solution.py:648

commit v8 on v7

--- a/solution.py
+++ b/solution.py
@@ -34,6 +34,7 @@
 UNROLL = 32
 CHAINS = 4
 FORCE_UNROLL = 8
+SEG_UNROLL = 16
 LOOP_UNROLL = 4
 EXTRA = 16
 VMEM_LIMIT = 32 << 20
@@ -63,7 +64,7 @@
             inside = (line >= q * depth) & (line < (q + 1) * depth)
             want = jnp.where(inside, (line + (depth0 - q * depth)) * CODE + (first + q), want)
         wants.append(want)
-    fills = (-1, LOWEST_FILL, -1, 0.0)
+    fills = (-1, LOWEST_FILL, -1)
 
     def pull(i, carry):
         parts = [list(part) for part in carry]
@@ -91,18 +92,16 @@
     start = (
         (jnp.full((SUB, LANES), LOWEST_FILL, jnp.float32),) * tiles,
         (jnp.full((SUB, LANES), KEY_LOW, jnp.int32),) * tiles,
-        (jnp.zeros((SUB, LANES), jnp.float32),) * tiles,
     )
 
     def one(j, carry):
-        pens, keys, gaps = (list(part) for part in carry)
-        slot, pen, key, gap = (row(ref, at + j) for ref in packs)
+        pens, keys = (list(part) for part in carry)
+        slot, pen, key = (row(ref, at + j) for ref in packs)
         for q in range(tiles):
             hit = slot == marks[q]
             pens[q] = jnp.maximum(pens[q], jnp.where(hit, pen, LOWEST_FILL))
             keys[q] = jnp.maximum(keys[q], jnp.where(hit, key, KEY_LOW))
-            gaps[q] = gaps[q] + jnp.where(hit, gap, 0.0)
-        return tuple(pens), tuple(keys), tuple(gaps)
+        return tuple(pens), tuple(keys)
 
     if unroll == depth:
         for j in range(depth):
@@ -119,12 +118,8 @@
 
 
 def across(accs):
-    pens, keys, gaps = (ref[...].T for ref in accs)
-    return (
-        jnp.max(pens, axis=0, keepdims=True),
-        jnp.max(keys, axis=0, keepdims=True),
-        jnp.sum(gaps, axis=0, keepdims=True),
-    )
+    pens, keys = (ref[...].T for ref in accs)
+    return jnp.max(pens, axis=0, keepdims=True), jnp.max(keys, axis=0, keepdims=True)
 
 
 def project(wt, x_ref, off_ref, tile):
@@ -155,7 +150,7 @@
 
 def prep_kernel(
     live_h, ns_h, nm_h, qw_h, sec_h, mst_h, off_h, jac_h, slot_h, face_h, rank_h,
-    x_ref, wt_ref, nq_ref, off_ref, jl_ref, slot_ref, code_ref, key_ref, over_pen, over_key, over_gap, area_ref,
+    x_ref, wt_ref, nq_ref, off_ref, jl_ref, slot_ref, code_ref, key_ref, over_pen, over_key, area_ref,
     live_s, ns_ref, nm_ref, qw_ref, jac_ref, face_ref, rank_ref, pen_ref, gap_ref, packs, accs, s_small, s_big,
 ):
     lines = slot_ref.shape[0]
@@ -227,7 +222,6 @@
     area_ref[...] = jnp.sum(jl, axis=0, keepdims=True) * jnp.sum(qrow, axis=1, keepdims=True)
     over_pen[...] = jnp.full(over_pen.shape, LOWEST_FILL, jnp.float32)
     over_key[...] = jnp.full(over_key.shape, KEY_LOW, jnp.int32)
-    over_gap[...] = jnp.zeros(over_gap.shape, jnp.float32)
 
     pltpu.make_async_copy(x_ref, x_ref, s_big).wait()
 
@@ -243,9 +237,7 @@
             tile = line // (TILE // LANES)
             reduce_field(project(weights, x_ref, off_ref, tile), p_size, tile, pen_ref, gap_ref)
             here = row(work, line) == mark
-            values = (
-                row(slot_ref, line), row(pen_ref, line), row(key_ref, line), row(gap_ref, line) * row(jl_ref, line)
-            )
+            values = (row(slot_ref, line), row(pen_ref, line), row(key_ref, line))
             for ref, value in zip(packs, values):
                 ref[0:SUB, :] = jnp.where(here, value, -1) if ref is packs[0] else value
             found = match_group(g, 0, 1, packs, 1)
@@ -253,13 +245,12 @@
             for side in range(PER_ROW):
                 keep_group(accs, side, [
                     [jnp.where(odd == side, x, fill) for x in part]
-                    for part, fill in zip(found, (LOWEST_FILL, KEY_LOW, 0.0))
+                    for part, fill in zip(found, (LOWEST_FILL, KEY_LOW))
                 ])
-            pen, key, gap = across(accs)
+            pen, key = across(accs)
             at = pl.ds(g // PER_ROW, 1)
             over_pen[at, :] = jnp.maximum(over_pen[at, :], pen)
             over_key[at, :] = jnp.maximum(over_key[at, :], key)
-            over_gap[at, :] = over_gap[at, :] + gap
             left = jnp.where(work[...] == mark, -1, work[...])
             work[...] = left
             return jnp.max(left)
@@ -269,11 +260,11 @@
 
 def main_kernel(
     n_dom, n_rep,
-    x_ref, wt_ref, nq_ref, off_ref, jl_ref, slot_ref, code_ref, key_ref, over_pen, over_key, over_gap, area_ref,
+    x_ref, wt_ref, nq_ref, off_ref, jl_ref, slot_ref, code_ref, key_ref, over_pen, over_key, area_ref,
     force_ref, out_pen, out_face, out_gap, out_mean,
-    load_ref, pen_ref, gap_ref, packs, even_accs, odd_accs, raw_pen, raw_key, raw_gap,
-    sp_sf, sp_si, ow_sf, ow_si, t1_s, t2_s, sp_f, sp_i, ow_f, ow_i, t1_d, t2_d,
-    s_spf, r_spf, s_spi, r_spi, s_owf, r_owf, s_owi, r_owi, s_t1, r_t1, s_t2, r_t2, inside,
+    load_ref, pen_ref, gap_ref, packs, even_accs, odd_accs, raw_pen, raw_key, seg_ref,
+    sp_sf, sp_sg, sp_si, ow_sf, ow_si, t1_s, t2_s, sp_f, sp_g, sp_i, ow_f, ow_i, t1_d, t2_d,
+    s_spf, r_spf, s_spg, r_spg, s_spi, r_spi, s_owf, r_owf, s_owi, r_owi, s_t1, r_t1, s_t2, r_t2, inside,
 ):
     dom = lax.axis_index("dom")
     rep = lax.axis_index("rep")
@@ -339,7 +330,7 @@
     signal(inside, 0, pair, 2, odd)
 
     def pull_batch(first):
-        pull_groups(first, BATCH, 0, DEPTH, code_ref, (slot_ref, pen_ref, key_ref, gap_ref), packs)
+        pull_groups(first, BATCH, 0, DEPTH, code_ref, (slot_ref, pen_ref, key_ref), packs)
 
     def match_pair(first, i, accs, last_accs, over, at):
         g = first + i * PER_ROW
@@ -349,11 +340,10 @@
         keep_group(accs, 1, match_group(g + 1, (i * PER_ROW + 1) * DEPTH, DEPTH, packs, DEPTH))
 
     def close_pair(accs, over, at):
-        pen, key, gap = across(accs)
+        pen, key = across(accs)
         over, at = pl.ds(over, 1), pl.ds(at, 1)
         raw_pen[at, :] = jnp.maximum(pen, over_pen[over, :])
         raw_key[at, :] = jnp.maximum(key, over_key[over, :])
-        raw_gap[at, :] = gap + over_gap[over, :]
 
     def decode(top, best):
         none = top < LOWEST_FILL * 0.5
@@ -367,8 +357,7 @@
     close_pair(odd_accs, OWN_ROWS + 1, 1)
     part = slice(0, SPILL_ROWS)
     rank, face = decode(raw_pen[part, :], raw_key[part, :])
-    sp_sf[0:SPILL_ROWS, :] = raw_pen[part, :]
-    sp_sf[SPILL_ROWS:, :] = raw_gap[part, :]
+    sp_sf[...] = raw_pen[part, :]
     sp_si[0:SPILL_ROWS, :] = rank
     sp_si[SPILL_ROWS:, :] = face
 
@@ -416,6 +405,30 @@
     quarter = lax.div(me * 4, count)
     turn = OWN_BATCHES - quarter - jnp.where(quarter >= 2, 1, 0)
 
+    hi_id = lax.broadcasted_iota(jnp.int32, (ALL_ROWS, TILE), 0)
+    lo_id = lax.broadcasted_iota(jnp.int32, (LANES, TILE), 0)
+
+    def total_up(step, total):
+        for i in range(SEG_UNROLL):
+            tile = step * SEG_UNROLL + i
+            slot = wide_row(slot_ref, tile)[0:1]
+            spread = jnp.where(hi_id == slot // LANES, wide_row(gap_ref, tile)[0:1], 0.0)
+            left = jnp.concatenate(split3(spread)[:2], axis=0)
+            right = jnp.where(lo_id == (slot & (LANES - 1)), 1.0, 0.0).astype(jnp.bfloat16)
+            total = total + lax.dot_general(
+                left, right, (((1,), (1,)), ((), ())), preferred_element_type=jnp.float32
+            )
+        return total
+
+    total = lax.fori_loop(0, tiles // SEG_UNROLL, total_up, jnp.zeros((2 * ALL_ROWS, LANES), jnp.float32))
+    seg_ref[...] = total[:ALL_ROWS] + total[ALL_ROWS:]
+    sp_sg[...] = seg_ref[OWN_ROWS : OWN_ROWS + SPILL_ROWS, :]
+    for j in range(n_rep):
+        pltpu.make_async_remote_copy(
+            src_ref=sp_sg, dst_ref=sp_g.at[rep], send_sem=s_spg, recv_sem=r_spg,
+            device_id=flat(dom + 1, rep + j), device_id_type=LOGICAL,
+        ).start()
+
     def own_scan(i, carry):
         @pl.when(i == turn)
         def _():
@@ -432,7 +445,7 @@
     close_pair(odd_accs, OWN_ROWS - 1, OWN_ROWS - 1)
     rank, face = decode(raw_pen[...], raw_key[...])
     ow_sf[0] = raw_pen[...]
-    ow_sf[1] = raw_gap[...]
+    ow_sf[1] = seg_ref[0:OWN_ROWS, :]
     ow_si[0] = rank
     ow_si[1] = face
 
@@ -488,6 +501,7 @@
         key_o = jnp.maximum(key_o, encode(ow_i[r, 0], ow_i[r, 1]))
 
     settle(sp_f, s_spf)
+    settle(sp_g, s_spg)
     settle(sp_i, s_spi)
     settle(ow_f.at[pl.ds(0, n_rep - 1)], s_owf)
     settle(ow_i.at[pl.ds(0, n_rep - 1)], s_owi)
@@ -496,16 +510,17 @@
 
     settle(t2_d.at[pl.ds(0, pairs - 1), :], r_t2)
     settle(sp_f, r_spf)
+    settle(sp_g, r_spg)
     settle(sp_i, r_spi)
     whole = jnp.sum(t2_d[...], axis=0, keepdims=True)
     out_mean[...] = whole[:, 0:1] / whole[:, 1:2]
 
     g = SPILL_ROWS
-    pen_s, gap_s = sp_f[0, 0:g], sp_f[0, g:]
+    pen_s, gap_s = sp_f[0], sp_g[0]
     key_s = encode(sp_i[0, 0:g], sp_i[0, g:])
     for r in range(1, n_rep):
-        pen_s = jnp.maximum(pen_s, sp_f[r, 0:g])
-        gap_s = gap_s + sp_f[r, g:]
+        pen_s = jnp.maximum(pen_s, sp_f[r])
+        gap_s = gap_s + sp_g[r]
         key_s = jnp.maximum(key_s, encode(sp_i[r, 0:g], sp_i[r, g:]))
 
     def finish(at, pen, key, gap):
@@ -559,10 +574,10 @@
         off, jac, slot, face, rank = (x.reshape(lines, LANES) for x in (off, jac, slot, face, rank))
 
         def packs(deep):
-            return [pltpu.VMEM((deep + SUB, LANES), t) for t in (i32, f32, i32, f32)]
+            return [pltpu.VMEM((deep + SUB, LANES), t) for t in (i32, f32, i32)]
 
         def lanes():
-            return [pltpu.VMEM((LANES, LANES), t) for t in (f32, i32, f32)]
+            return [pltpu.VMEM((LANES, LANES), t) for t in (f32, i32)]
 
         held = pl.pallas_call(
             prep_kernel,
@@ -577,11 +592,10 @@
                 pltpu.VMEM((lines, LANES), i32),
                 pltpu.VMEM((ALL_ROWS, LANES), f32),
                 pltpu.VMEM((ALL_ROWS, LANES), i32),
-                pltpu.VMEM((ALL_ROWS, LANES), f32),
                 pltpu.VMEM((1, LANES), f32),
             ),
             in_specs=[anywhere] * 11,
-            out_specs=(vmem,) * 12,
+            out_specs=(vmem,) * 11,
             scratch_shapes=[
                 pltpu.VMEM((1, 1), i32),
                 pltpu.VMEM((k_size, p_size), bf16),
@@ -615,7 +629,7 @@
                 pltpu.VMEM((OWN_ROWS, LANES), f32),
                 pltpu.VMEM((1, 1), f32),
             ),
-            in_specs=[vmem] * 12,
+            in_specs=[vmem] * 11,
             out_specs=(vmem,) * 5,
             scratch_shapes=[
                 pltpu.VMEM((p_size, rows), bf16),
@@ -626,20 +640,22 @@
                 lanes(),
                 pltpu.VMEM((OWN_ROWS, LANES), f32),
                 pltpu.VMEM((OWN_ROWS, LANES), i32),
-                pltpu.VMEM((OWN_ROWS, LANES), f32),
-                pltpu.VMEM(spill, f32),
+                pltpu.VMEM((ALL_ROWS, LANES), f32),
+                pltpu.VMEM((SPILL_ROWS, LANES), f32),
+                pltpu.VMEM((SPILL_ROWS, LANES), f32),
                 pltpu.VMEM(spill, i32),
                 pltpu.VMEM(own, f32),
                 pltpu.VMEM(own, i32),
                 pltpu.VMEM((1, LANES), f32),
                 pltpu.VMEM((1, LANES), f32),
-                pltpu.VMEM((n_rep,) + spill, f32),
+                pltpu.VMEM((n_rep, SPILL_ROWS, LANES), f32),
+                pltpu.VMEM((n_rep, SPILL_ROWS, LANES), f32),
                 pltpu.VMEM((n_rep,) + spill, i32),
                 pltpu.VMEM((n_rep,) + own, f32),
                 pltpu.VMEM((n_rep,) + own, i32),
                 pltpu.VMEM((1, LANES), f32),
                 pltpu.VMEM((pairs, LANES), f32),
-            ] + [dma] * 12 + [pltpu.SemaphoreType.REGULAR],
+            ] + [dma] * 14 + [pltpu.SemaphoreType.REGULAR],
             compiler_params=pltpu.CompilerParams(
                 collective_id=0, has_side_effects=True, vmem_limit_bytes=VMEM_LIMIT
             ),

time: 16.9 us -> 17.6 us (1.041)
  Pallas kernels: 15.4 us -> 16.1 us
    pallas_call x1, Pallas kernels: 12.1 us -> 12.8 us  [shards(): pl.pallas_call(functools.partial(main_kernel, n_dom, n_rep), out_shape=(p...]
where the time goes in v8:
time: 17.6 us; the launch traced here: 17.4 us
  Pallas kernels  16.1 us (91%)
  between operations  1.3 us (7%)
    pallas_call x1, Pallas kernels, shards(): pl.pallas_call(functools.partial(main_kernel, n_dom, n_rep), out_shape=(p...  12.8 us
    pallas_call x1, Pallas kernels, shards(): pl.pallas_call(prep_kernel, out_shape=(pltpu.VMEM((2 * k_size, rows), bf1...  1.71 us
    pallas_call x1, Pallas kernels, shards(): pl.pallas_call(finish_kernel, out_shape=tuple((jax.ShapeDtypeStruct(x.sha...  1.64 us

profile of v8, /device:TPU:0, one launch (start us, length us, event | category | flops | bytes accessed | tf_op | source)
XLA Modules:
  0.0 17.4 jit_solution(3720922917518841697)
XLA Ops:
  1.3 1.7 %shard_map.146 = (bf16[128,8192]{1,0:T(8,128)(2,1)S(1)}, bf16[272,144]{1,0:T(8,128)(2,1)S(1)}, bf16[128,256]{1,0:T(8,128)(2,1)S(1)}, f32[64,128]{1,0:T(8,128)S(1...) custom-call(s32[1,1]{1,0:T(1,128)} %bitcast.11.live_h, ...), custom_call_target="tpu_custom_call" | custom-call | tf_op jit(solution)/shard_map/pallas_call | solution.py:582
  3.0 12.8 %shard_map.147 = (bf16[64,8192]{1,0:T(8,128)(2,1)S(1)}, f32[8,128]{1,0:T(8,128)S(1)}, s32[8,128]{1,0:T(8,128)S(1)}, f32[8,128]{1,0:T(8,128)S(1)}, f32[1,1]{1,0:T(1,128)}) custom-call(bf16[128,8192]{1,0:T(8,128)(2,1)S(1)} %get-tuple-element.26.x_ref, bf16[272,144]{1,0:T(8,128)(2,1)S(1)} %get-tuple-element.27.wt_ref, ...), custom_call_target="tpu_custom_call" | custom-call | tf_op jit(solution)/shard_map/pallas_call | solution.py:623
  15.8 1.6 %shard_map.148 = (bf16[64,8192]{1,0:T(8,128)(2,1)}, f32[8,128]{1,0:T(8,128)}, s32[8,128]{1,0:T(8,128)}, f32[8,128]{1,0:T(8,128)}, f32[1,1]{1,0:T(1,128)}) custom-call(bf16[64,8192]{1,0:T(8,128)(2,1)S(1)} %get-tuple-element.37.force_ref, f32[8,128]{1,0:T(8,128)S(1)} %get-tuple-element.38.pen_ref, s32[8,128]{1,0:T(8,128)S(1)} %get-tuple-element.39.face_ref, ...), custom_call_target="tpu_custom_call" | custom-call | tf_op jit(solution)/shard_map/pallas_call | solution.py:664

commit v9 on v7

--- a/solution.py
+++ b/solution.py
@@ -327,7 +327,8 @@
     total_gap = jnp.sum(jnp.sum(row_gap, axis=0, keepdims=True), axis=1, keepdims=True)
     total_area = jnp.sum(area_ref[...], axis=1, keepdims=True)
     lane = lax.broadcasted_iota(jnp.int32, (1, LANES), 1)
-    t1_s[...] = jnp.where(lane == 0, total_gap, jnp.where(lane == 1, total_area, 0.0))
+    t1_s[0:1, :] = jnp.where(lane == 0, total_gap, 0.0)
+    t1_s[1:2, :] = jnp.where(lane == 0, total_area, 1.0)
 
     after = n_rep * jnp.where(dom == n_dom - 1, 0, 1)
     pl.semaphore_wait(barrier, me + (n_rep - 1 - rep) + after)
@@ -346,7 +347,8 @@
         keep_group(accs, 0, match_group(g, i * PER_ROW * DEPTH, DEPTH, packs, LOOP_UNROLL))
         if last_accs is not None:
             close_pair(last_accs, over, at)
-        keep_group(accs, 1, match_group(g + 1, (i * PER_ROW + 1) * DEPTH, DEPTH, packs, DEPTH))
+        unroll = LOOP_UNROLL if last_accs is None else DEPTH
+        keep_group(accs, 1, match_group(g + 1, (i * PER_ROW + 1) * DEPTH, DEPTH, packs, unroll))
 
     def close_pair(accs, over, at):
         pen, key, gap = across(accs)
@@ -392,12 +394,12 @@
     first_copy.wait_recv()
     both = t1_s[...] + t1_d[...]
     t2_s[...] = both
-    t2_d[pl.ds(pair, 1), :] = both
+    t2_d[pair] = both
 
     def send_pairs(first, last):
         def one(other, carry):
             pltpu.make_async_remote_copy(
-                src_ref=t2_s, dst_ref=t2_d.at[pl.ds(pair, 1), :], send_sem=s_t2, recv_sem=r_t2,
+                src_ref=t2_s, dst_ref=t2_d.at[pair], send_sem=s_t2, recv_sem=r_t2,
                 device_id=other * 2 + odd, device_id_type=LOGICAL,
             ).start()
             return carry
@@ -492,13 +494,13 @@
     settle(ow_f.at[pl.ds(0, n_rep - 1)], s_owf)
     settle(ow_i.at[pl.ds(0, n_rep - 1)], s_owi)
     first_copy.wait_send()
-    settle(t2_d.at[pl.ds(0, pairs - 1), :], s_t2)
-
-    settle(t2_d.at[pl.ds(0, pairs - 1), :], r_t2)
+    settle(t2_d.at[pl.ds(0, pairs - 1)], s_t2)
+
+    settle(t2_d.at[pl.ds(0, pairs - 1)], r_t2)
     settle(sp_f, r_spf)
     settle(sp_i, r_spi)
-    whole = jnp.sum(t2_d[...], axis=0, keepdims=True)
-    out_mean[...] = whole[:, 0:1] / whole[:, 1:2]
+    whole = jnp.sum(t2_d[...], axis=0)
+    out_mean[...] = (whole[0:1] / whole[1:2])[:, 0:1]
 
     g = SPILL_ROWS
     pen_s, gap_s = sp_f[0, 0:g], sp_f[0, g:]
@@ -631,14 +633,14 @@
                 pltpu.VMEM(spill, i32),
                 pltpu.VMEM(own, f32),
                 pltpu.VMEM(own, i32),
-                pltpu.VMEM((1, LANES), f32),
-                pltpu.VMEM((1, LANES), f32),
+                pltpu.VMEM((2, LANES), f32),
+                pltpu.VMEM((2, LANES), f32),
                 pltpu.VMEM((n_rep,) + spill, f32),
                 pltpu.VMEM((n_rep,) + spill, i32),
                 pltpu.VMEM((n_rep,) + own, f32),
                 pltpu.VMEM((n_rep,) + own, i32),
-                pltpu.VMEM((1, LANES), f32),
-                pltpu.VMEM((pairs, LANES), f32),
+                pltpu.VMEM((2, LANES), f32),
+                pltpu.VMEM((pairs, 2, LANES), f32),
             ] + [dma] * 12 + [pltpu.SemaphoreType.REGULAR],
             compiler_params=pltpu.CompilerParams(
                 collective_id=0, has_side_effects=True, vmem_limit_bytes=VMEM_LIMIT

time: 16.9 us -> 16.8 us (level)
  no operation moved by 1% of the time
where the time goes in v9:
time: 16.8 us; the launch traced here: 16.6 us
  Pallas kernels  15.3 us (91%)
  between operations  1.3 us (8%)
    pallas_call x1, Pallas kernels, shards(): pl.pallas_call(functools.partial(main_kernel, n_dom, n_rep), out_shape=(p...  12 us
    pallas_call x1, Pallas kernels, shards(): pl.pallas_call(prep_kernel, out_shape=(pltpu.VMEM((2 * k_size, rows), bf1...  1.71 us
    pallas_call x1, Pallas kernels, shards(): pl.pallas_call(finish_kernel, out_shape=tuple((jax.ShapeDtypeStruct(x.sha...  1.64 us

profile of v9, /device:TPU:0, one launch (start us, length us, event | category | flops | bytes accessed | tf_op | source)
XLA Modules:
  0.0 16.6 jit_solution(1022197991411532530)
XLA Ops:
  1.3 1.7 %shard_map.146 = (bf16[128,8192]{1,0:T(8,128)(2,1)S(1)}, bf16[272,144]{1,0:T(8,128)(2,1)S(1)}, bf16[128,256]{1,0:T(8,128)(2,1)S(1)}, f32[64,128]{1,0:T(8,128)S(1...) custom-call(s32[1,1]{1,0:T(1,128)} %bitcast.11.live_h, ...), custom_call_target="tpu_custom_call" | custom-call | tf_op jit(solution)/shard_map/pallas_call | solution.py:569
  3.0 12.0 %shard_map.147 = (bf16[64,8192]{1,0:T(8,128)(2,1)S(1)}, f32[8,128]{1,0:T(8,128)S(1)}, s32[8,128]{1,0:T(8,128)S(1)}, f32[8,128]{1,0:T(8,128)S(1)}, f32[1,1]{1,0:T(1,128)}) custom-call(bf16[128,8192]{1,0:T(8,128)(2,1)S(1)} %get-tuple-element.27.x_ref, bf16[272,144]{1,0:T(8,128)(2,1)S(1)} %get-tuple-element.28.wt_ref, ...), custom_call_target="tpu_custom_call" | custom-call | tf_op jit(solution)/shard_map/pallas_call | solution.py:611
  15.0 1.6 %shard_map.148 = (bf16[64,8192]{1,0:T(8,128)(2,1)}, f32[8,128]{1,0:T(8,128)}, s32[8,128]{1,0:T(8,128)}, f32[8,128]{1,0:T(8,128)}, f32[1,1]{1,0:T(1,128)}) custom-call(bf16[64,8192]{1,0:T(8,128)(2,1)S(1)} %get-tuple-element.39.force_ref, f32[8,128]{1,0:T(8,128)S(1)} %get-tuple-element.40.pen_ref, s32[8,128]{1,0:T(8,128)S(1)} %get-tuple-element.41.face_ref, ...), custom_call_target="tpu_custom_call" | custom-call | tf_op jit(solution)/shard_map/pallas_call | solution.py:650

commit v10 on v9

--- a/solution.py
+++ b/solution.py
@@ -337,7 +337,8 @@
         device_id=flat(dom, mate), device_id_type=LOGICAL,
     )
     first_copy.start()
-    signal(inside, 0, pair, 2, odd)
+    last_dom = dom == n_dom - 1
+    signal(inside, 0, jnp.where(last_dom, 0, pair), 2, odd)
 
     def pull_batch(first):
         pull_groups(first, BATCH, 0, DEPTH, code_ref, (slot_ref, pen_ref, key_ref, gap_ref), packs)
@@ -391,6 +392,7 @@
         for copy in spill_copy(j):
             copy.start()
 
+    signal(inside, 0, jnp.where(last_dom, pair, 0), 2, odd)
     first_copy.wait_recv()
     both = t1_s[...] + t1_d[...]
     t2_s[...] = both

time: 16.8 us -> 17 us (1.012)
  the two profiles are of different devices: /device:TPU:0 before, /device:TPU:17 now
where the time goes in v10:
time: 17 us; the launch traced here: 16.9 us
  Pallas kernels  15.6 us (92%)
  between operations  1.3 us (8%)
    pallas_call x1, Pallas kernels, shards(): pl.pallas_call(functools.partial(main_kernel, n_dom, n_rep), out_shape=(p...  12.2 us
    pallas_call x1, Pallas kernels, shards(): pl.pallas_call(prep_kernel, out_shape=(pltpu.VMEM((2 * k_size, rows), bf1...  1.71 us
    pallas_call x1, Pallas kernels, shards(): pl.pallas_call(finish_kernel, out_shape=tuple((jax.ShapeDtypeStruct(x.sha...  1.64 us

profile of v10, /device:TPU:17, one launch (start us, length us, event | category | flops | bytes accessed | tf_op | source)
XLA Modules:
  0.0 16.9 jit_solution(8957259201158808992)
XLA Ops:
  1.3 1.7 %shard_map.146 = (bf16[128,8192]{1,0:T(8,128)(2,1)S(1)}, bf16[272,144]{1,0:T(8,128)(2,1)S(1)}, bf16[128,256]{1,0:T(8,128)(2,1)S(1)}, f32[64,128]{1,0:T(8,128)S(1...) custom-call(s32[1,1]{1,0:T(1,128)} %bitcast.11.live_h, ...), custom_call_target="tpu_custom_call" | custom-call | tf_op jit(solution)/shard_map/pallas_call | solution.py:571
  3.0 12.2 %shard_map.147 = (bf16[64,8192]{1,0:T(8,128)(2,1)S(1)}, f32[8,128]{1,0:T(8,128)S(1)}, s32[8,128]{1,0:T(8,128)S(1)}, f32[8,128]{1,0:T(8,128)S(1)}, f32[1,1]{1,0:T(1,128)}) custom-call(bf16[128,8192]{1,0:T(8,128)(2,1)S(1)} %get-tuple-element.27.x_ref, bf16[272,144]{1,0:T(8,128)(2,1)S(1)} %get-tuple-element.28.wt_ref, ...), custom_call_target="tpu_custom_call" | custom-call | tf_op jit(solution)/shard_map/pallas_call | solution.py:613
  15.2 1.6 %shard_map.148 = (bf16[64,8192]{1,0:T(8,128)(2,1)}, f32[8,128]{1,0:T(8,128)}, s32[8,128]{1,0:T(8,128)}, f32[8,128]{1,0:T(8,128)}, f32[1,1]{1,0:T(1,128)}) custom-call(bf16[64,8192]{1,0:T(8,128)(2,1)S(1)} %get-tuple-element.39.force_ref, f32[8,128]{1,0:T(8,128)S(1)} %get-tuple-element.40.pen_ref, s32[8,128]{1,0:T(8,128)S(1)} %get-tuple-element.41.face_ref, ...), custom_call_target="tpu_custom_call" | custom-call | tf_op jit(solution)/shard_map/pallas_call | solution.py:652
